TPU v7x, 128 devices: a whole 4x4x4 slice. The times are simulated.
128 devices in a mesh: slab: 16 (over z, y), sub: 8 (over x, core).
Axes of the slice: x: 4, y: 4, z: 4, core: 2. Of those that a mesh axis runs over, the one named last changes fastest.
Arguments:
- velocity: float32 [65536, 3, 128], P(('slab', 'sub')), may hold values from -6 to 6
- weight: float32 [65536, 128], P(('slab', 'sub')), may hold values from 0.2 to 2
- offset: int32 [65536, 128], P(('slab', 'sub')), may hold values from 0 to 127
- owner: int32 [65536, 1], P(('slab', 'sub')), may hold values from 0 to 127; in each aligned block of 512 rows (0 to 511, 512 to 1023, ...) at most 8 rows name the same one
- brick: int32 [65536, 1], P(('slab', 'sub')), may hold values from 0 to 4095
- flags: int32 [128, 512, 1024], P('slab', 'sub'), may hold values from 0 to 2, as said below
Outputs:
- updated: float32 [65536, 3, 128], P(('slab', 'sub'))
- pressure: float32 [128, 512, 1024], P('slab', 'sub')
- solved_face_velocity: float32 [3, 128, 512, 1024], P(None, 'slab', 'sub')
Inputs may be any that keep to these rules, and one draw needn't show every extreme that they name: Among the blocks of one device, at most 8 name the same owner. `flags`: 0 air, 1 liquid, 2 solid.
All inputs are finite; a program needn't handle non-finite values.
Results may differ from a plain program's by a relative error of at most 0.000075.
Values sent between devices are 32-bit elements; how exact they have to be, the bound alone decides.
No kernel may reach another device: no remote copies, remote signals or barrier semaphores. Data moves between devices by JAX's collectives and lax.ppermute only.
A program may use at most 128 MiB of HBM per device.

v0:
```python
import functools
import jax
import jax.numpy as jnp
from jax import lax
from jax.experimental import pallas as pl
from jax.experimental.pallas import tpu as pltpu
from jax.sharding import PartitionSpec as P

F32 = jnp.float32
BF16 = jnp.bfloat16
I32 = jnp.int32
LANES = 128
CHUNK = 33
COLUMN = 33
MIB = 1 << 20


def vmem():
    return pl.BlockSpec(memory_space=pltpu.VMEM)


def smem():
    return pl.BlockSpec(memory_space=pltpu.SMEM)


def call(kernel, ins, outs, shapes, scratch=(), limit=16, flops=2_000_000, **kw):
    return pl.pallas_call(
        kernel,
        in_specs=ins,
        out_specs=outs,
        out_shape=shapes,
        scratch_shapes=list(scratch),
        compiler_params=pltpu.CompilerParams(vmem_limit_bytes=limit * MIB),
        cost_estimate=pl.CostEstimate(flops=flops, bytes_accessed=1 << 20, transcendentals=0),
        **kw,
    )


def two_parts(x):
    high = x.astype(BF16).astype(F32)
    return high, x - high


def one_hot(offsets, cells):
    return jnp.where(jnp.broadcast_to(offsets, cells.shape) == cells, 1.0, 0.0).astype(BF16)


def splat_kernel(vel, weight, offset, owner, brick, out, place, parts, names, count):
    blocks = weight.shape[0]
    devices = names.shape[0]
    out[...] = jnp.zeros_like(out)
    names[...] = jnp.full(names.shape, 4096.0, F32)

    def clear(d, carry):
        count[d] = 0
        return carry

    lax.fori_loop(0, devices, clear, 0, unroll=8)

    def load(g, carry):
        rows = pl.ds(pl.multiple_of(g * 8, 8), 8)
        w = weight[rows, :]
        base = pl.multiple_of(g * 128, 128)
        for c in range(4):
            high, low = two_parts(vel[c, rows, :] * w if c < 3 else w)
            parts[pl.ds(base + c, 8, stride=16), :] = high
            parts[pl.ds(base + 8 + c, 8, stride=16), :] = low
        return carry

    lax.fori_loop(0, blocks // 8, load, 0, unroll=2)
    cells = lax.broadcasted_iota(I32, (LANES, LANES), 0)
    lane = lax.broadcasted_iota(I32, (1, LANES), 1)
    many = 8

    def step(g, carry):
        base = pl.multiple_of(g * many, many)
        offs = offset[pl.ds(base, many), :]
        sums = []
        for j in range(many):
            hot = one_hot(offs[j : j + 1, :], cells)
            lhs = parts[pl.ds(pl.multiple_of(base * 16, 128) + 16 * j, 16), :].astype(BF16)
            r = lax.dot_general(lhs, hot, (((1,), (1,)), ((), ())), preferred_element_type=F32)
            sums.append(r[0:8] + r[8:16])
        for j in range(many):
            d = owner[base + j]
            slot = count[d]
            count[d] = slot + 1
            place[base + j] = d * 8 + slot
            out[pl.ds(d * CHUNK + slot * 4, 4), :] = sums[j][0:4]
            b = brick[base + j]
            old = names[pl.ds(d, 1), :]
            names[pl.ds(d, 1), :] = jnp.where(lane == slot, jnp.full((1, LANES), b, I32).astype(F32), old)
        return carry

    lax.fori_loop(0, blocks // many, step, 0)
    out[pl.ds(32, devices, stride=CHUNK), :] = names[...]


def splat(vel, weight, offset, owner, brick, devices):
    blocks = weight.shape[0]
    return call(
        splat_kernel,
        [vmem()] * 3 + [smem()] * 2,
        [vmem(), smem()],
        [jax.ShapeDtypeStruct((devices * CHUNK, LANES), F32), jax.ShapeDtypeStruct((blocks,), I32)],
        [pltpu.VMEM((blocks * 16, LANES), F32), pltpu.VMEM((devices, LANES), F32), pltpu.SMEM((devices,), I32)],
    )(vel, weight, offset, owner, brick)


def pick_kernel(ret, vel, offset, place, out, parts, sums):
    blocks = offset.shape[0]
    cells = lax.broadcasted_iota(I32, (LANES, LANES), 0)
    many = 8

    def gather(g, carry):
        base = pl.multiple_of(g * 8, 8)
        for j in range(8):
            x = ret[pl.ds(place[base + j] * 3, 3), :]
            high, low = two_parts(x)
            at = pl.multiple_of(base * 16, 128) + 16 * j
            parts[pl.ds(at, 3), :] = high
            parts[pl.ds(at + 8, 3), :] = low
        return carry

    lax.fori_loop(0, blocks // 8, gather, 0)

    def step(g, carry):
        base = pl.multiple_of(g * many, many)
        offs = offset[pl.ds(base, many), :]
        for j in range(many):
            hot = one_hot(offs[j : j + 1, :], cells)
            lhs = parts[pl.ds(pl.multiple_of(base * 16, 128) + 16 * j, 16), :].astype(BF16)
            r = lax.dot_general(lhs, hot, (((1,), (0,)), ((), ())), preferred_element_type=F32)
            sums[pl.ds(pl.multiple_of(base * 8, 64) + 8 * j, 8), :] = r[0:8] + r[8:16]
        return carry

    lax.fori_loop(0, blocks // many, step, 0)

    def add(g, carry):
        rows = pl.ds(pl.multiple_of(g * 8, 8), 8)
        for c in range(3):
            out[c, rows, :] = vel[c, rows, :] + sums[pl.ds(pl.multiple_of(g * 64, 64) + c, 8, stride=8), :]
        return carry

    lax.fori_loop(0, blocks // 8, add, 0, unroll=4)


def pick(ret, vel, offset, place):
    blocks = offset.shape[0]
    return call(
        pick_kernel,
        [vmem()] * 3 + [smem()],
        vmem(),
        jax.ShapeDtypeStruct((3, blocks, LANES), F32),
        [pltpu.VMEM((blocks * 16, LANES), F32), pltpu.VMEM((blocks * 8, LANES), F32)],
    )(ret, vel, offset, place)


def scatter_kernel(arr, names, tot, first, last):
    xs, ys = first.shape[0] // 96, 64
    per = 8 * CHUNK

    def clear(g, carry):
        tot[pl.ds(pl.multiple_of(g * 8, 8), 8), :] = jnp.zeros((8, LANES), F32)
        return carry

    lax.fori_loop(0, tot.shape[0] // 8, clear, 0, unroll=16)

    def step(g, carry):
        base = pl.multiple_of(g * per, 8)
        for k in range(64):
            b = names[g * 64 + k]
            row = (b >> 3) * COLUMN + (b & 7) * 4
            at = pl.ds(row, 4)
            tot[at, :] = tot[at, :] + arr[pl.ds(base + (k // 8) * CHUNK + (k % 8) * 4, 4), :]
        return carry

    lax.fori_loop(0, arr.shape[0] // per, step, 0)
    for x in range(xs):
        for r in range(3):
            first[pl.ds(x * 96 + r * 32, 32), :] = tot[pl.ds((x * ys + r) * COLUMN, 32), :]
            last[pl.ds(x * 96 + r * 32, 32), :] = tot[pl.ds((x * ys + ys - 3 + r) * COLUMN, 32), :]


def scatter(arr, names, xs, ys):
    rows = xs * ys * COLUMN + 8
    halo = jax.ShapeDtypeStruct((xs * 96, LANES), F32)
    return call(
        scatter_kernel,
        [vmem(), smem()],
        [vmem()] * 3,
        [jax.ShapeDtypeStruct((rows, LANES), F32), halo, halo],
    )(arr, names)
ROWS = 72
FACE_X, FACE_Y, FACE_Z, LIQUID = 1, 2, 4, 8
STEP = 0.15


def strip(z):
    return pl.ds(z * LANES, LANES)


def lanes():
    return lax.broadcasted_iota(I32, (ROWS, LANES), 1)


def before_y(a):
    return pltpu.roll(a, 1, 0)


def after_y(a):
    return pltpu.roll(a, ROWS - 1, 0)


def before_z(strips):
    lane = lanes()
    rolled = [pltpu.roll(a, 1, 1) for a in strips]
    return [jnp.where(lane == 0, rolled[z - 1], rolled[z]) for z in range(len(strips))]


def after_z(strips):
    lane = lanes()
    rolled = [pltpu.roll(a, LANES - 1, 1) for a in strips]
    last = len(strips) - 1
    return [jnp.where(lane == LANES - 1, rolled[z + 1 if z < last else 0], rolled[z]) for z in range(len(strips))]


def strips_of(ref, index, count):
    return [ref[(*index, slice(None), strip(z))] for z in range(count)]


def code_kernel(flags, tile, beyond, code):
    xs, zs = code.shape[0], code.shape[2] // LANES

    def encoded(x):
        def one(z):
            f = flags[x, :, strip(z)]
            return jnp.concatenate([jnp.where(f == 2, 0, f + 1), tile[x, :, strip(z)]], 0)

        return [one(z) for z in range(zs)]

    def layer(x, e, e_next):
        o = [jnp.minimum(a, 1) for a in e]
        o_z = after_z(o)
        lane = lanes()
        o_z[-1] = jnp.where(lane == LANES - 1, 0, o_z[-1])
        for z in range(zs):
            c = o[z] & jnp.minimum(e_next[z], 1)
            c = c | ((o[z] & after_y(o[z])) << 1) | ((o[z] & o_z[z]) << 2)
            code[x, :, strip(z)] = c | jnp.where(e[z] == 2, LIQUID, 0)

    def step(x, carry):
        layer(x, encoded(x), encoded(x + 1))
        return carry

    lax.fori_loop(0, xs - 1, step, 0)
    layer(xs - 1, encoded(xs - 1), strips_of(beyond, (), zs))


def make_code(flags, tile, beyond):
    xs, _, nz = flags.shape
    return call(
        code_kernel, [vmem()] * 3, vmem(), jax.ShapeDtypeStruct((xs, ROWS, nz), I32)
    )(flags, tile, beyond)


def partial_spread(v, x, zs):
    vx, vy, vz = (strips_of(v, (a, x), zs) for a in range(3))
    vz_before = before_z(vz)
    return [vx[z] + (vy[z] - before_y(vy[z])) + (vz[z] - vz_before[z]) for z in range(zs)]


def send_layers(v, to_next, to_prior, xs, zs):
    for z, s in enumerate(partial_spread(v, 0, zs)):
        to_prior[:, strip(z)] = s
    to_next[...] = v[0, xs - 1]


def fields_kernel(tot, after, prior, code, guess, inverse, v, to_next, to_prior, edge):
    xs, ys, zs = code.shape[0], ROWS - 8, code.shape[2] // LANES
    for x in range(xs):
        edge[pl.ds(x * 256, 96), :] = after[pl.ds(x * 96, 96), :]
        edge[pl.ds(x * 256 + 96, 64), :] = jnp.zeros((64, LANES), F32)
        edge[pl.ds(x * 256 + 160, 96), :] = prior[pl.ds(x * 96, 96), :]

    def step(x, carry):
        for z in range(zs):
            def read(c):
                rows = [
                    tot[pl.ds((x * ys + y * 8) * COLUMN + z * 4 + c, 8, stride=COLUMN), :]
                    for y in range(ys // 8)
                ]
                rows.append(edge[pl.ds(x * 256 + z * 4 + c, 8, stride=32), :])
                return jnp.concatenate(rows, 0)

            r = 1.0 / (read(3) + 1.0)
            inverse[x, :, strip(z)] = r
            bits = code[x, :, strip(z)]
            for a in range(3):
                g = read(a) * r
                guess[a, x, :, strip(z)] = g
                v[a, x, :, strip(z)] = jnp.where(bits & (1 << a) != 0, g, 0.0)
        return carry

    lax.fori_loop(0, xs, step, 0)
    send_layers(v, to_next, to_prior, xs, zs)


def fields(tot, after, prior, code):
    xs, _, nz = code.shape
    one = jax.ShapeDtypeStruct((xs, ROWS, nz), F32)
    three = jax.ShapeDtypeStruct((3, xs, ROWS, nz), F32)
    layer = jax.ShapeDtypeStruct((ROWS, nz), F32)
    return call(
        fields_kernel,
        [vmem()] * 4,
        [vmem()] * 5,
        [three, one, three, layer, layer],
        [pltpu.VMEM((xs * 256, LANES), F32)],
    )(tot, after, prior, code)


def ascend(p_out, p_in, v, code, x, before, first, zs):
    spread = partial_spread(v, x, zs)
    for z in range(zs):
        s = spread[z] - before(z)
        old = -STEP * s if first else p_in[x, :, strip(z)] - STEP * s
        liquid = code[x, :, strip(z)] & LIQUID != 0
        p_out[x, :, strip(z)] = jnp.where(liquid, jnp.maximum(old, 0.0), 0.0)


def push(v_out, p, code, guess, inverse, x, after, zs):
    here = strips_of(p, (x,), zs)
    here_z = after_z(here)
    for z in range(zs):
        r = inverse[x, :, strip(z)]
        bits = code[x, :, strip(z)]
        beyond = (after(z), after_y(here[z]), here_z[z])
        for a in range(3):
            moved = guess[a, x, :, strip(z)] + (here[z] - beyond[a]) * r
            v_out[a, x, :, strip(z)] = jnp.where(bits & (1 << a) != 0, moved, 0.0)


def inner_kernel(first, p_in, v_in, code, guess, inverse, p, v):
    xs, zs = code.shape[0], code.shape[2] // LANES

    def up(x, carry):
        ascend(p, p_in, v_in, code, x, lambda z: v_in[0, x - 1, :, strip(z)], first, zs)
        return carry

    lax.fori_loop(1, xs, up, 0)

    def out(x, carry):
        push(v, p, code, guess, inverse, x, lambda z: p[x + 1, :, strip(z)], zs)
        return carry

    lax.fori_loop(1, xs - 1, out, 0)


def outer_kernel(first, before, spread, beyond, p8_in, p_in, v_in, code, guess, inverse, p, v, p8, to_next, to_prior):
    xs, zs = code.shape[0], code.shape[2] // LANES
    ascend(p, p_in, v_in, code, 0, lambda z: before[:, strip(z)], first, zs)
    for z in range(zs):
        s = spread[:, strip(z)] - v_in[0, xs - 1, :, strip(z)]
        old = -STEP * s if first else p8_in[:, strip(z)] - STEP * s
        p8[:, strip(z)] = jnp.where(beyond[:, strip(z)] == 2, jnp.maximum(old, 0.0), 0.0)
    push(v, p, code, guess, inverse, 0, lambda z: p[1, :, strip(z)], zs)
    push(v, p, code, guess, inverse, xs - 1, lambda z: p8[:, strip(z)], zs)
    send_layers(v, to_next, to_prior, xs, zs)


def inner(first, p, v, code, guess, inverse):
    shapes = [jax.ShapeDtypeStruct(a.shape, F32) for a in (p, v)]
    return call(
        functools.partial(inner_kernel, first),
        [vmem()] * 5,
        [vmem()] * 2,
        shapes,
        input_output_aliases={0: 0, 1: 1},
    )(p, v, code, guess, inverse)


def outer(first, before, spread, beyond, p8, p, v, code, guess, inverse):
    shapes = [jax.ShapeDtypeStruct(a.shape, F32) for a in (p, v, p8, p8, p8)]
    return call(
        functools.partial(outer_kernel, first),
        [vmem()] * 9,
        [vmem()] * 5,
        shapes,
        input_output_aliases={4: 0, 5: 1},
    )(before, spread, beyond, p8, p, v, code, guess, inverse)


def reply_kernel(v, guess, names, reply, change):
    xs, ys, zs = v.shape[1], ROWS - 8, v.shape[3] // LANES

    def turn(x, carry):
        for a in range(3):
            for z in range(zs):
                for y in range(ys // 8):
                    at = (a, x, slice(y * 8, y * 8 + 8), strip(z))
                    change[pl.ds((x * ys + y * 8) * COLUMN + z * 4 + a, 8, stride=COLUMN), :] = v[at] - guess[at]
        return carry

    lax.fori_loop(0, xs, turn, 0)

    def step(g, carry):
        base = pl.multiple_of(g * 192, 192)
        for k in range(64):
            b = names[g * 64 + k]
            reply[pl.ds(base + 3 * k, 3), :] = change[pl.ds((b >> 3) * COLUMN + (b & 7) * 4, 3), :]
        return carry

    lax.fori_loop(0, reply.shape[0] // 192, step, 0)


def make_reply(v, guess, names):
    xs = v.shape[1]
    return call(
        reply_kernel,
        [vmem()] * 2 + [smem()],
        vmem(),
        jax.ShapeDtypeStruct((names.shape[0] * 3, LANES), F32),
        [pltpu.VMEM((xs * (ROWS - 8) * COLUMN + 8, LANES), F32)],
    )(v, guess, names)


def shifted(block, axis, distance):
    devices = range(lax.axis_size(axis))
    return lax.ppermute(block, axis, [(i - distance, i) for i in devices if i - distance in devices])


ITERS = 3


def on_device(velocity, weight, offset, owner, brick, flags):
    devices = lax.axis_size("slab") * lax.axis_size("sub")
    xs, ys, nz = flags.shape
    both = ("slab", "sub")
    kinds = jnp.where(flags == 2, 0, flags + 1)
    later = shifted(kinds[:, :4], "sub", -1)
    prior = shifted(kinds[:, ys - 3 :], "sub", 1)
    tile = jnp.concatenate([later, jnp.zeros((xs, 1, nz), I32), prior], 1)
    beyond = shifted(jnp.concatenate([kinds[0], tile[0]], 0), "slab", -1)
    planes = velocity.transpose(1, 0, 2)
    outgoing, place = splat(planes, weight, offset, owner[:, 0], brick[:, 0], devices)
    arrived = lax.all_to_all(outgoing.reshape(devices, 1, CHUNK * LANES), both, 0, 0, tiled=True)
    code = make_code(flags, tile, beyond)
    names = arrived[:, 0, 32 * LANES : 32 * LANES + 8].astype(I32).reshape(-1)
    totals, first_rows, last_rows = scatter(arrived.reshape(devices * CHUNK, LANES), names, xs, ys)
    after = shifted(first_rows, "sub", -1)
    before = shifted(last_rows, "sub", 1)
    guess, inverse, v, to_next, to_prior = fields(totals, after, before, code)
    p = jnp.zeros((xs, ROWS, nz), F32)
    p8 = jnp.zeros((ROWS, nz), F32)
    for sweep in range(ITERS):
        from_prior = shifted(to_next, "slab", 1)
        from_next = shifted(to_prior, "slab", -1)
        p, v = inner(sweep == 0, p, v, code, guess, inverse)
        p, v, p8, to_next, to_prior = outer(
            sweep == 0, from_prior, from_next, beyond, p8, p, v, code, guess, inverse
        )
    reply = make_reply(v, guess, names)
    back = lax.all_to_all(reply.reshape(devices, 24, LANES), both, 0, 0, tiled=True)
    updated = pick(back.reshape(devices * 24, LANES), planes, offset, place)
    return updated.transpose(1, 0, 2), p[:, :ys], v[:, :, :ys]


def solution(mesh):
    return jax.shard_map(
        on_device,
        mesh=mesh,
        in_specs=(P(("slab", "sub")),) * 5 + (P("slab", "sub"),),
        out_specs=(P(("slab", "sub")), P("slab", "sub"), P(None, "slab", "sub")),
        check_vma=False,
    )
```

profile of v0, /device:TPU:1, one launch (start us, length us, event | category | flops | bytes accessed | tf_op | source)
XLA Modules:
  0.0 199.7 jit_solution(4277091466429057924)
XLA Ops:
  5.0 18.4 %shard_map.85 = (f32[4224,128]{1,0:T(8,128)S(1)}, s32[512]{0:T(512)S(1)}) custom-call(f32[3,512,128]{2,1,0:T(8,128)S(1)} %bitcast.15, f32[512,128]{1,0:T(8,128)S(1)} %copy-done.10, s32[512,128]{1,0:T(8,128)S(1)} %copy-done.8, s32[512]{0:T(512)S(1)} %bitcast.18, s32[512]{0:T(512)S(1)} %bitcast.19), custom_call_target="tpu_custom_call" | custom-call | flops 2000000 | bytes 1048576 | tf_op jit(solution)/shard_map/pallas_call | solution.py:101
  23.5 1.3 copy-done.7
  24.8 11.5 %all-to-all-start = ((f32[128,1,4224]{2,1,0:T(1,128)}), f32[128,1,4224]{2,1,0:T(1,128)S(1)}, u32[]{:S(2)}, u32[]{:S(2)}) async-start(f32[128,1,4224]{2,1,0:T(1,128)} %bitcast.17), calls=%async_computation | async-start | bytes 4325376 | tf_op jit(solution)/shard_map/all_to_all | solution.py:447
  36.3 1.9 add_select_fusion
  38.2 3.0 %collective-permute-start.2 = (s32[8,4,1024]{2,1,0:T(4,128)S(1)}, s32[8,4,1024]{2,1,0:T(4,128)S(1)}, u32[]{:S(2)}, u32[]{:S(2)}) collective-permute-start(s32[8,4,1024]{2,1,0:T(4,128)S(1)} %slice.29), channel_id=1, source_target_pairs={{1,0},{2,1},{3,2},{4,3},{5,4},{6,5},{7,6},{9,8},{10,9},{11,10},{12... | collective-permute-start | bytes 393224 | tf_op jit(solution)/shard_map/ppermute | solution.py:430
  41.2 2.6 %collective-permute-start.3 = (s32[8,3,1024]{2,1,0:T(4,128)S(1)}, s32[8,3,1024]{2,1,0:T(4,128)S(1)}, u32[]{:S(2)}, u32[]{:S(2)}) collective-permute-start(s32[8,3,1024]{2,1,0:T(4,128)S(1)} %slice.30), channel_id=1, source_target_pairs={{0,1},{1,2},{2,3},{3,4},{4,5},{5,6},{6,7},{8,9},{9,10},{10,11},{11... | collective-permute-start | bytes 294920 | tf_op jit(solution)/shard_map/ppermute | solution.py:430
  44.6 16.1 %collective-permute-done.3 = s32[8,3,1024]{2,1,0:T(4,128)S(1)} collective-permute-done((s32[8,3,1024]{2,1,0:T(4,128)S(1)}, s32[8,3,1024]{2,1,0:T(4,128)S(1)}, u32[]{:S(2)}, u32[]{:S(2)}) %collective-permute-start.3) | collective-permute-done | bytes 98336 | tf_op jit(solution)/shard_map/ppermute | solution.py:430
  60.8 2.1 %collective-permute-done.2 = s32[8,4,1024]{2,1,0:T(4,128)S(1)} collective-permute-done((s32[8,4,1024]{2,1,0:T(4,128)S(1)}, s32[8,4,1024]{2,1,0:T(4,128)S(1)}, u32[]{:S(2)}, u32[]{:S(2)}) %collective-permute-start.2) | collective-permute-done | bytes 131104 | tf_op jit(solution)/shard_map/ppermute | solution.py:430
  62.9 4.5 %all-to-all-done = f32[128,1,4224]{2,1,0:T(1,128)S(1)} async-done(((f32[128,1,4224]{2,1,0:T(1,128)}), f32[128,1,4224]{2,1,0:T(1,128)S(1)}, u32[]{:S(2)}, u32[]{:S(2)}) %all-to-all-start) | async-done | bytes 2162720 | tf_op jit(solution)/shard_map/all_to_all | solution.py:447
  67.8 6.7 %shard_map.86 = (f32[16904,128]{1,0:T(8,128)S(1)}, f32[768,128]{1,0:T(8,128)S(1)}, f32[768,128]{1,0:T(8,128)S(1)}) custom-call(f32[4224,128]{1,0:T(8,128)S(1)} %bitcast.13, s32[1024]{0:T(1024)S(1)} %convert_element_type.8.names), custom_call_target="tpu_custom_call" | custom-call | flops 2000000 | bytes 1048576 | tf_op jit(solution)/shard_map/pallas_call | solution.py:188
  74.5 3.4 %copy-done.1 = f32[16904,128]{1,0:T(8,128)} copy-done((f32[16904,128]{1,0:T(8,128)}, f32[16904,128]{1,0:T(8,128)S(1)}, u32[]{:S(2)}) %copy-start.1) | copy-done | bytes 8654872
  77.9 3.4 %collective-permute-start = (f32[768,128]{1,0:T(8,128)S(1)}, f32[768,128]{1,0:T(8,128)S(1)}, u32[]{:S(2)}, u32[]{:S(2)}) collective-permute-start(f32[768,128]{1,0:T(8,128)S(1)} %get-tuple-element.33), channel_id=1, source_target_pairs={{1,0},{2,1},{3,2},{4,3},{5,4},{6,5},{7,6},{9,8},{10,9},{11,10},{12... | collective-permute-start | bytes 1179656 | tf_op jit(solution)/shard_map/ppermute | solution.py:430
  81.3 2.1 %collective-permute-start.1 = (f32[768,128]{1,0:T(8,128)S(1)}, f32[768,128]{1,0:T(8,128)S(1)}, u32[]{:S(2)}, u32[]{:S(2)}) collective-permute-start(f32[768,128]{1,0:T(8,128)S(1)} %get-tuple-element.34), channel_id=1, source_target_pairs={{0,1},{1,2},{2,3},{3,4},{4,5},{5,6},{6,7},{8,9},{9,10},{10,11},{11... | collective-permute-start | bytes 1179656 | tf_op jit(solution)/shard_map/ppermute | solution.py:430
  85.7 8.9 %collective-permute-done.4.beyond = s32[72,1024]{1,0:T(8,128)S(1)} collective-permute-done((s32[72,1024]{1,0:T(8,128)S(1)}, s32[72,1024]{1,0:T(8,128)S(1)}, u32[]{:S(2)}, u32[]{:S(2)}) %collective-permute-start.4) | collective-permute-done | bytes 294944 | tf_op jit(solution)/shard_map/ppermute | solution.py:430
  94.6 1.8 shard_map.87.code
  96.5 3.4 %copy-done.2 = f32[16904,128]{1,0:T(8,128)S(1)} copy-done((f32[16904,128]{1,0:T(8,128)S(1)}, f32[16904,128]{1,0:T(8,128)}, u32[]{:S(2)}) %copy-start.2) | copy-done | bytes 8654872
  99.9 2.9 %shard_map.88 = (f32[3,8,72,1024]{3,2,1,0:T(8,128)S(1)}, f32[8,72,1024]{2,1,0:T(8,128)S(1)}, f32[3,8,72,1024]{3,2,1,0:T(8,128)S(1)}, f32[72,1024]{1,0:T(8,128)S(1)}, f32[72,1024]{1,0:T(8,128)S(1)}) custom-call(f32[16904,128]{1,0:T(8,128)S(1)} %copy-done.2, f32[768,128]{1,0:T(8,128)S(1)} %collective-permute-done.after, ...), custom_call_target="tpu_custom_call" | custom-call | flops 2000000 | bytes 1048576 | tf_op jit(solution)/shard_map/pallas_call | solution.py:314
  105.7 2.8 %shard_map.89 = (f32[8,72,1024]{2,1,0:T(8,128)S(1)}, f32[3,8,72,1024]{3,2,1,0:T(8,128)S(1)}) custom-call(f32[8,72,1024]{2,1,0:T(8,128)S(1)} %broadcast_in_dim.16.p_in, f32[3,8,72,1024]{3,2,1,0:T(8,128)S(1)} %get-tuple-element.37.v_in, s32[8,72,1024]{2,1,0:T(8,128)S(1)} %shard_map.87.code, ...), custom_call_target="tpu_custom_call", output_to_operand_aliasing={{0}: (0, {}), {1}: (1, {})} | custom-call | flops 2000000 | bytes 1048576 | tf_op jit(solution)/shard_map/pallas_call | solution.py:374
  109.4 3.8 %collective-permute-done.6.spread = f32[72,1024]{1,0:T(8,128)S(1)} collective-permute-done((f32[72,1024]{1,0:T(8,128)S(1)}, f32[72,1024]{1,0:T(8,128)S(1)}, u32[]{:S(2)}, u32[]{:S(2)}) %collective-permute-start.6) | collective-permute-done | bytes 294944 | tf_op jit(solution)/shard_map/ppermute | solution.py:430
  114.2 6.1 %collective-permute-start.7 = (f32[72,1024]{1,0:T(8,128)S(1)}, f32[72,1024]{1,0:T(8,128)S(1)}, u32[]{:S(2)}, u32[]{:S(2)}) collective-permute-start(f32[72,1024]{1,0:T(8,128)S(1)} %get-tuple-element.42), channel_id=1, source_target_pairs={{0,8},{8,16},{16,24},{24,32},{32,40},{40,48},{48,56},{56,64},{64,7... | collective-permute-start | bytes 884744 | tf_op jit(solution)/shard_map/ppermute | solution.py:430
  121.6 3.0 %shard_map.91 = (f32[8,72,1024]{2,1,0:T(8,128)S(1)}, f32[3,8,72,1024]{3,2,1,0:T(8,128)S(1)}) custom-call(f32[8,72,1024]{2,1,0:T(8,128)S(1)} %get-tuple-element.45.p_in, f32[3,8,72,1024]{3,2,1,0:T(8,128)S(1)} %get-tuple-element.46.v_in, s32[8,72,1024]{2,1,0:T(8,128)S(1)} %shard_map.87.code, ...), custom_call_target="tpu_custom_call", output_to_operand_aliasing={{0}: (0, {}), {1}: (1, {})} | custom-call | flops 2000000 | bytes 1048576 | tf_op jit(solution)/shard_map/pallas_call | solution.py:374
  125.4 3.9 %collective-permute-done.8.spread = f32[72,1024]{1,0:T(8,128)S(1)} collective-permute-done((f32[72,1024]{1,0:T(8,128)S(1)}, f32[72,1024]{1,0:T(8,128)S(1)}, u32[]{:S(2)}, u32[]{:S(2)}) %collective-permute-start.8) | collective-permute-done | bytes 294944 | tf_op jit(solution)/shard_map/ppermute | solution.py:430
  130.3 4.3 %collective-permute-start.9 = (f32[72,1024]{1,0:T(8,128)S(1)}, f32[72,1024]{1,0:T(8,128)S(1)}, u32[]{:S(2)}, u32[]{:S(2)}) collective-permute-start(f32[72,1024]{1,0:T(8,128)S(1)} %get-tuple-element.49), channel_id=1, source_target_pairs={{0,8},{8,16},{16,24},{24,32},{32,40},{40,48},{48,56},{56,64},{64,7... | collective-permute-start | bytes 884744 | tf_op jit(solution)/shard_map/ppermute | solution.py:430
  135.9 3.0 %shard_map.93 = (f32[8,72,1024]{2,1,0:T(8,128)S(1)}, f32[3,8,72,1024]{3,2,1,0:T(8,128)S(1)}) custom-call(f32[8,72,1024]{2,1,0:T(8,128)S(1)} %get-tuple-element.52.p_in, f32[3,8,72,1024]{3,2,1,0:T(8,128)S(1)} %get-tuple-element.53.v_in, s32[8,72,1024]{2,1,0:T(8,128)S(1)} %shard_map.87.code, ...), custom_call_target="tpu_custom_call", output_to_operand_aliasing={{0}: (0, {}), {1}: (1, {})} | custom-call | flops 2000000 | bytes 1048576 | tf_op jit(solution)/shard_map/pallas_call | solution.py:374
  138.9 3.8 %collective-permute-done.10.spread = f32[72,1024]{1,0:T(8,128)S(1)} collective-permute-done((f32[72,1024]{1,0:T(8,128)S(1)}, f32[72,1024]{1,0:T(8,128)S(1)}, u32[]{:S(2)}, u32[]{:S(2)}) %collective-permute-start.10) | collective-permute-done | bytes 294944 | tf_op jit(solution)/shard_map/ppermute | solution.py:430
  142.7 1.9 shard_map.94
  144.5 3.5 %shard_map.95 = f32[3072,128]{1,0:T(8,128)S(1)} custom-call(f32[3,8,72,1024]{3,2,1,0:T(8,128)S(1)} %get-tuple-element.56.v, f32[3,8,72,1024]{3,2,1,0:T(8,128)S(1)} %get-tuple-element.38.guess, s32[1024]{0:T(1024)S(1)} %convert_element_type.8.names), custom_call_target="tpu_custom_call" | custom-call | flops 2000000 | bytes 1048576 | tf_op jit(solution)/shard_map/pallas_call | solution.py:419
  149.2 10.6 %all-to-all-start.1 = ((f32[128,24,128]{2,1,0:T(8,128)}), f32[128,24,128]{2,1,0:T(8,128)}, u32[]{:S(2)}, u32[]{:S(2)}) async-start(f32[128,24,128]{2,1,0:T(8,128)} %bitcast.14), calls=%async_computation.1 | async-start | bytes 3145728 | tf_op jit(solution)/shard_map/all_to_all | solution.py:464
  159.8 6.6 %slice.27 = f32[3,8,64,1024]{3,2,1,0:T(8,128)} slice(f32[3,8,72,1024]{3,2,1,0:T(8,128)} %copy-done), slice={[0:3], [0:8], [0:64], [0:1024]} | slice | bytes 12582912 | tf_op jit(solution)/shard_map/slice | solution.py:466
  166.5 1.5 slice.26
  167.9 16.5 %all-to-all-done.1 = f32[128,24,128]{2,1,0:T(8,128)} async-done(((f32[128,24,128]{2,1,0:T(8,128)}), f32[128,24,128]{2,1,0:T(8,128)}, u32[]{:S(2)}, u32[]{:S(2)}) %all-to-all-start.1) | async-done | bytes 1572896 | tf_op jit(solution)/shard_map/all_to_all | solution.py:464
  184.4 15.3 %shard_map.96 = f32[3,512,128]{2,1,0:T(8,128)} custom-call(f32[3072,128]{1,0:T(8,128)} %bitcast.8.ret, f32[3,512,128]{2,1,0:T(8,128)S(1)} %bitcast.16, s32[512,128]{1,0:T(8,128)S(1)} %copy-done.9, s32[512]{0:T(512)S(1)} %get-tuple-element.57.place), custom_call_target="tpu_custom_call" | custom-call | flops 2000000 | bytes 1048576 | tf_op jit(solution)/shard_map/pallas_call | solution.py:150
  (46 shorter events, 18.2 us)
Async XLA Ops:
  0.6 1.1 copy-start.5
  1.8 0.9 copy-start.8
  2.7 0.9 copy-start.10
  3.7 0.7 copy-start.11
  4.4 0.7 copy-start.12
  23.5 1.3 copy-start.7
  24.8 42.7 %all-to-all-start = ((f32[128,1,4224]{2,1,0:T(1,128)}), f32[128,1,4224]{2,1,0:T(1,128)S(1)}, u32[]{:S(2)}, u32[]{:S(2)}) async-start(f32[128,1,4224]{2,1,0:T(1,128)} %bitcast.17), calls=%async_computation | async-start | bytes 4325376 | tf_op jit(solution)/shard_map/all_to_all | solution.py:447
  38.2 24.6 %collective-permute-start.2 = (s32[8,4,1024]{2,1,0:T(4,128)S(1)}, s32[8,4,1024]{2,1,0:T(4,128)S(1)}, u32[]{:S(2)}, u32[]{:S(2)}) collective-permute-start(s32[8,4,1024]{2,1,0:T(4,128)S(1)} %slice.29), channel_id=1, source_target_pairs={{1,0},{2,1},{3,2},{4,3},{5,4},{6,5},{7,6},{9,8},{10,9},{11,10},{12... | collective-permute-start | bytes 393224 | tf_op jit(solution)/shard_map/ppermute | solution.py:430
  41.2 19.5 %collective-permute-start.3 = (s32[8,3,1024]{2,1,0:T(4,128)S(1)}, s32[8,3,1024]{2,1,0:T(4,128)S(1)}, u32[]{:S(2)}, u32[]{:S(2)}) collective-permute-start(s32[8,3,1024]{2,1,0:T(4,128)S(1)} %slice.30), channel_id=1, source_target_pairs={{0,1},{1,2},{2,3},{3,4},{4,5},{5,6},{6,7},{8,9},{9,10},{10,11},{11... | collective-permute-start | bytes 294920 | tf_op jit(solution)/shard_map/ppermute | solution.py:430
  67.8 26.8 %copy-start.3 = (s32[8,64,1024]{2,1,0:T(8,128)S(1)}, s32[8,64,1024]{2,1,0:T(8,128)}, u32[]{:S(2)}) copy-start(s32[8,64,1024]{2,1,0:T(8,128)} %flags.1) | copy-start | bytes 6291460
  74.5 3.4 %copy-start.1 = (f32[16904,128]{1,0:T(8,128)}, f32[16904,128]{1,0:T(8,128)S(1)}, u32[]{:S(2)}) copy-start(f32[16904,128]{1,0:T(8,128)S(1)} %get-tuple-element.32.tot) | copy-start | bytes 25964548
  77.9 18.6 %collective-permute-start = (f32[768,128]{1,0:T(8,128)S(1)}, f32[768,128]{1,0:T(8,128)S(1)}, u32[]{:S(2)}, u32[]{:S(2)}) collective-permute-start(f32[768,128]{1,0:T(8,128)S(1)} %get-tuple-element.33), channel_id=1, source_target_pairs={{1,0},{2,1},{3,2},{4,3},{5,4},{6,5},{7,6},{9,8},{10,9},{11,10},{12... | collective-permute-start | bytes 1179656 | tf_op jit(solution)/shard_map/ppermute | solution.py:430
  81.3 15.2 %collective-permute-start.1 = (f32[768,128]{1,0:T(8,128)S(1)}, f32[768,128]{1,0:T(8,128)S(1)}, u32[]{:S(2)}, u32[]{:S(2)}) collective-permute-start(f32[768,128]{1,0:T(8,128)S(1)} %get-tuple-element.34), channel_id=1, source_target_pairs={{0,1},{1,2},{2,3},{3,4},{4,5},{5,6},{6,7},{8,9},{9,10},{10,11},{11... | collective-permute-start | bytes 1179656 | tf_op jit(solution)/shard_map/ppermute | solution.py:430
  84.4 10.2 %collective-permute-start.4 = (s32[72,1024]{1,0:T(8,128)S(1)}, s32[72,1024]{1,0:T(8,128)S(1)}, u32[]{:S(2)}, u32[]{:S(2)}) collective-permute-start(s32[72,1024]{1,0:T(8,128)S(1)} %pad_add_fusion), channel_id=1, source_target_pairs={{8,0},{16,8},{24,16},{32,24},{40,32},{48,40},{56,48},{64,56},{72,6... | collective-permute-start | bytes 884744 | tf_op jit(solution)/shard_map/ppermute | solution.py:430
  96.4 3.5 %copy-start.2 = (f32[16904,128]{1,0:T(8,128)S(1)}, f32[16904,128]{1,0:T(8,128)}, u32[]{:S(2)}) copy-start(f32[16904,128]{1,0:T(8,128)} %copy-done.1) | copy-start | bytes 25964548
  102.8 6.6 %collective-permute-start.5 = (f32[72,1024]{1,0:T(8,128)S(1)}, f32[72,1024]{1,0:T(8,128)S(1)}, u32[]{:S(2)}, u32[]{:S(2)}) collective-permute-start(f32[72,1024]{1,0:T(8,128)S(1)} %get-tuple-element.35), channel_id=1, source_target_pairs={{0,8},{8,16},{16,24},{24,32},{32,40},{40,48},{48,56},{56,64},{64,7... | collective-permute-start | bytes 884744 | tf_op jit(solution)/shard_map/ppermute | solution.py:430
  104.1 9.2 %collective-permute-start.6 = (f32[72,1024]{1,0:T(8,128)S(1)}, f32[72,1024]{1,0:T(8,128)S(1)}, u32[]{:S(2)}, u32[]{:S(2)}) collective-permute-start(f32[72,1024]{1,0:T(8,128)S(1)} %get-tuple-element.36), channel_id=1, source_target_pairs={{8,0},{16,8},{24,16},{32,24},{40,32},{48,40},{56,48},{64,56},{72,6... | collective-permute-start | bytes 884744 | tf_op jit(solution)/shard_map/ppermute | solution.py:430
  114.2 11.2 %collective-permute-start.7 = (f32[72,1024]{1,0:T(8,128)S(1)}, f32[72,1024]{1,0:T(8,128)S(1)}, u32[]{:S(2)}, u32[]{:S(2)}) collective-permute-start(f32[72,1024]{1,0:T(8,128)S(1)} %get-tuple-element.42), channel_id=1, source_target_pairs={{0,8},{8,16},{16,24},{24,32},{32,40},{40,48},{48,56},{56,64},{64,7... | collective-permute-start | bytes 884744 | tf_op jit(solution)/shard_map/ppermute | solution.py:430
  120.3 8.9 %collective-permute-start.8 = (f32[72,1024]{1,0:T(8,128)S(1)}, f32[72,1024]{1,0:T(8,128)S(1)}, u32[]{:S(2)}, u32[]{:S(2)}) collective-permute-start(f32[72,1024]{1,0:T(8,128)S(1)} %get-tuple-element.43), channel_id=1, source_target_pairs={{8,0},{16,8},{24,16},{32,24},{40,32},{48,40},{56,48},{64,56},{72,6... | collective-permute-start | bytes 884744 | tf_op jit(solution)/shard_map/ppermute | solution.py:430
  130.3 8.6 %collective-permute-start.9 = (f32[72,1024]{1,0:T(8,128)S(1)}, f32[72,1024]{1,0:T(8,128)S(1)}, u32[]{:S(2)}, u32[]{:S(2)}) collective-permute-start(f32[72,1024]{1,0:T(8,128)S(1)} %get-tuple-element.49), channel_id=1, source_target_pairs={{0,8},{8,16},{16,24},{24,32},{32,40},{40,48},{48,56},{56,64},{64,7... | collective-permute-start | bytes 884744 | tf_op jit(solution)/shard_map/ppermute | solution.py:430
  134.6 8.1 %collective-permute-start.10 = (f32[72,1024]{1,0:T(8,128)S(1)}, f32[72,1024]{1,0:T(8,128)S(1)}, u32[]{:S(2)}, u32[]{:S(2)}) collective-permute-start(f32[72,1024]{1,0:T(8,128)S(1)} %get-tuple-element.50), channel_id=1, source_target_pairs={{8,0},{16,8},{24,16},{32,24},{40,32},{48,40},{56,48},{64,56},{72,6... | collective-permute-start | bytes 884744 | tf_op jit(solution)/shard_map/ppermute | solution.py:430
  144.5 3.5 %copy-start = (f32[3,8,72,1024]{3,2,1,0:T(8,128)}, f32[3,8,72,1024]{3,2,1,0:T(8,128)S(1)}, u32[]{:S(2)}) copy-start(f32[3,8,72,1024]{3,2,1,0:T(8,128)S(1)} %get-tuple-element.56.v) | copy-start | bytes 21233668
  148.1 1.1 copy-start.4
  149.2 35.2 %all-to-all-start.1 = ((f32[128,24,128]{2,1,0:T(8,128)}), f32[128,24,128]{2,1,0:T(8,128)}, u32[]{:S(2)}, u32[]{:S(2)}) async-start(f32[128,24,128]{2,1,0:T(8,128)} %bitcast.14), calls=%async_computation.1 | async-start | bytes 3145728 | tf_op jit(solution)/shard_map/all_to_all | solution.py:464
  166.5 17.9 %copy-start.6 = (f32[512,3,128]{2,0,1:T(8,128)S(1)}, f32[512,3,128]{2,0,1:T(8,128)}, u32[]{:S(2)}) copy-start(f32[512,3,128]{2,0,1:T(8,128)} %param.6) | copy-start | bytes 2359300
  166.5 17.9 %copy-start.9 = (s32[512,128]{1,0:T(8,128)S(1)}, s32[512,128]{1,0:T(8,128)}, u32[]{:S(2)}) copy-start(s32[512,128]{1,0:T(8,128)} %offset.3) | copy-start | bytes 786436
where the time goes:
time: 201 us; the launch traced here: 200 us
  Pallas kernels  61.3 us (30%)
  waiting for transfers between devices  61.3 us (30%)
  starting transfers between devices  50.1 us (25%)
  local copies, waits for them, and re-layouts  23 us (11%)
  other arithmetic  3.11 us (2%)
    ppermute x11, waiting for transfers between devices, shifted(): lax.ppermute(block, axis, [(i - distance, i) for i in devices if i - dist...  40.3 us
    ppermute x11, starting transfers between devices, shifted(): lax.ppermute(block, axis, [(i - distance, i) for i in devices if i - dist...  28 us
    pallas_call x1, Pallas kernels, splat(): call(splat_kernel, [vmem()] * 3 + [smem()] * 2, [vmem(), smem()], [jax.Sh...  18.4 us
    all_to_all x1, waiting for transfers between devices, on_device(): lax.all_to_all(reply.reshape(devices, 24, LANES), both, 0, 0, tiled=True)  16.5 us
    pallas_call x1, Pallas kernels, pick(): call(pick_kernel, [vmem()] * 3 + [smem()], vmem(), jax.ShapeDtypeStruct((...  15.3 us
    unnamed x26, local copies, waits for them, and re-layouts  13.7 us
    all_to_all x1, starting transfers between devices, on_device(): lax.all_to_all(outgoing.reshape(devices, 1, CHUNK * LANES), both, 0, 0, t...  11.5 us
    all_to_all x1, starting transfers between devices, on_device(): lax.all_to_all(reply.reshape(devices, 24, LANES), both, 0, 0, tiled=True)  10.6 us
  transfers between devices with their start and end apart: 13, of which 10 were waited for; matrix products, arithmetic and copies ran while one was open for 6% of the time, Pallas kernels for 5%

commit v1 on v0

v1 whole, which is shorter than its diff:
```python
import functools
import jax
import jax.numpy as jnp
from jax import lax
from jax.experimental import pallas as pl
from jax.experimental.pallas import tpu as pltpu
from jax.sharding import PartitionSpec as P

F32 = jnp.float32
BF16 = jnp.bfloat16
I32 = jnp.int32
LANES = 128
CHUNK = 33
COLUMN = 33
MIB = 1 << 20
GROUP = 64


def vmem():
    return pl.BlockSpec(memory_space=pltpu.VMEM)


def hbm():
    return pl.BlockSpec(memory_space=pltpu.HBM)


def smem():
    return pl.BlockSpec(memory_space=pltpu.SMEM)


def call(kernel, ins, outs, shapes, scratch=(), limit=3, micros=3, **kw):
    return pl.pallas_call(
        kernel,
        in_specs=ins,
        out_specs=outs,
        out_shape=shapes,
        scratch_shapes=list(scratch),
        compiler_params=pltpu.CompilerParams(vmem_limit_bytes=limit * MIB),
        cost_estimate=pl.CostEstimate(flops=micros * 100_000_000, bytes_accessed=1 << 20, transcendentals=0),
        **kw,
    )


def two_parts(x):
    high = x.astype(BF16).astype(F32)
    return high, x - high


def one_hot(offsets, cells):
    return jnp.where(jnp.broadcast_to(offsets, cells.shape) == cells, 1.0, 0.0).astype(BF16)


def splat_kernel(
    vel_hbm, weight_hbm, offset_hbm, owner_hbm, brick_hbm, out, place,
    vel, weight, offset, owner, brick, parts, names, count, sems
):
    pairs = ((vel_hbm, vel), (weight_hbm, weight), (offset_hbm, offset), (owner_hbm, owner), (brick_hbm, brick))
    copies = [pltpu.make_async_copy(a, b, sems.at[i]) for i, (a, b) in enumerate(pairs)]
    for copy in copies:
        copy.start()
    blocks = weight.shape[0]
    devices = names.shape[0]
    names[...] = jnp.full(names.shape, 4096.0, F32)

    def clear(g, carry):
        out[pl.ds(pl.multiple_of(g * 8, 8), 8), :] = jnp.zeros((8, LANES), F32)
        return carry

    lax.fori_loop(0, out.shape[0] // 8, clear, 0, unroll=16)

    def reset(d, carry):
        count[d] = 0
        return carry

    lax.fori_loop(0, devices, reset, 0, unroll=8)
    for copy in copies:
        copy.wait()

    def load(g, carry):
        for half in range(2):
            rows = pl.ds(pl.multiple_of(g * 16 + 8 * half, 8), 8)
            w = weight[rows, :]
            base = pl.multiple_of(g * 128, 128) + 4 * half
            for c in range(4):
                high, low = two_parts(vel[c, rows, :] * w if c < 3 else w)
                parts[pl.ds(base + c, 8, stride=16), :] = high
                parts[pl.ds(base + 8 + c, 8, stride=16), :] = low
        return carry

    lax.fori_loop(0, blocks // 16, load, 0, unroll=2)
    cells = lax.broadcasted_iota(I32, (LANES, LANES), 0)
    lane = lax.broadcasted_iota(I32, (1, LANES), 1)
    upper = lax.broadcasted_iota(I32, (16, LANES), 0) % 8 < 4

    def step(g, carry):
        base = pl.multiple_of(g * GROUP, GROUP)
        offs = offset[pl.ds(base, GROUP), :]
        sums = [None] * GROUP
        for t in range(GROUP // 16):
            for q in range(8):
                one, two = t * 16 + q, t * 16 + 8 + q
                hot = jnp.concatenate(
                    [one_hot(offs[one : one + 1, :], cells), one_hot(offs[two : two + 1, :], cells)], 1
                )
                x = parts[pl.ds(pl.multiple_of(base * 8, 8 * GROUP) + 128 * t + 16 * q, 16), :]
                lhs = jnp.concatenate([jnp.where(upper, x, 0.0), jnp.where(upper, 0.0, x)], 1).astype(BF16)
                r = lax.dot_general(lhs, hot, (((1,), (1,)), ((), ())), preferred_element_type=F32)
                r = r[0:8] + r[8:16]
                sums[one], sums[two] = r[0:4], r[4:8]
        for j in range(GROUP):
            d = owner[base + j]
            slot = count[d]
            count[d] = slot + 1
            place[base + j] = d * 8 + slot
            out[pl.ds(d * CHUNK + slot * 4, 4), :] = sums[j]
            b = brick[base + j]
            old = names[pl.ds(d, 1), :]
            names[pl.ds(d, 1), :] = jnp.where(lane == slot, jnp.full((1, LANES), b, I32).astype(F32), old)
        return carry

    lax.fori_loop(0, blocks // GROUP, step, 0)
    out[pl.ds(32, devices, stride=CHUNK), :] = names[...]


def splat(vel, weight, offset, owner, brick, devices):
    blocks = weight.shape[0]
    return call(
        splat_kernel,
        [hbm()] * 5,
        [vmem(), smem()],
        [jax.ShapeDtypeStruct((devices * CHUNK, LANES), F32), jax.ShapeDtypeStruct((blocks,), I32)],
        [
            pltpu.VMEM(vel.shape, F32),
            pltpu.VMEM(weight.shape, F32),
            pltpu.VMEM(offset.shape, I32),
            pltpu.SMEM((blocks,), I32),
            pltpu.SMEM((blocks,), I32),
            pltpu.VMEM((blocks * 8, LANES), F32),
            pltpu.VMEM((devices, LANES), F32),
            pltpu.SMEM((devices,), I32),
            pltpu.SemaphoreType.DMA((5,)),
        ],
        limit=60,
        micros=8,
    )(vel, weight, offset, owner, brick)


def pick_kernel(ret, vel, offset, place, out, parts, sums):
    blocks = offset.shape[0]
    cells = lax.broadcasted_iota(I32, (LANES, LANES), 0)
    upper = lax.broadcasted_iota(I32, (8, LANES), 0) < 4

    def gather(g, carry):
        base = pl.multiple_of(g * 16, 16)
        for j in range(16):
            high, low = two_parts(ret[pl.ds(place[base + j] * 3, 3), :])
            at = pl.multiple_of(base * 8, 128) + 16 * (j % 8) + 4 * (j // 8)
            parts[pl.ds(at, 3), :] = high
            parts[pl.ds(at + 8, 3), :] = low
        return carry

    lax.fori_loop(0, blocks // 16, gather, 0)

    def step(g, carry):
        base = pl.multiple_of(g * GROUP, GROUP)
        offs = offset[pl.ds(base, GROUP), :]
        for t in range(GROUP // 16):
            for q in range(8):
                one, two = t * 16 + q, t * 16 + 8 + q
                hot = jnp.concatenate(
                    [one_hot(offs[one : one + 1, :], cells), one_hot(offs[two : two + 1, :], cells)], 1
                )
                lhs = parts[pl.ds(pl.multiple_of(base * 8, 8 * GROUP) + 128 * t + 16 * q, 16), :].astype(BF16)
                r = lax.dot_general(lhs, hot, (((1,), (0,)), ((), ())), preferred_element_type=F32)
                r = r[0:8] + r[8:16]
                at = pl.multiple_of(base * 4, 4 * GROUP) + 64 * t + 8 * q
                sums[pl.ds(at, 8), :] = jnp.where(upper, r[:, :LANES], r[:, LANES:])
        return carry

    lax.fori_loop(0, blocks // GROUP, step, 0)

    def add(g, carry):
        for half in range(2):
            rows = pl.ds(pl.multiple_of(g * 16 + 8 * half, 8), 8)
            for c in range(3):
                change = sums[pl.ds(pl.multiple_of(g * 64, 64) + 4 * half + c, 8, stride=8), :]
                out[c, rows, :] = vel[c, rows, :] + change
        return carry

    lax.fori_loop(0, blocks // 16, add, 0, unroll=4)


def pick(ret, vel, offset, place):
    blocks = offset.shape[0]
    return call(
        pick_kernel,
        [vmem()] * 3 + [smem()],
        vmem(),
        jax.ShapeDtypeStruct((3, blocks, LANES), F32),
        [pltpu.VMEM((blocks * 8, LANES), F32), pltpu.VMEM((blocks * 4, LANES), F32)],
        limit=12,
        micros=6,
    )(ret, vel, offset, place)


def scatter_kernel(arr_hbm, names, tot, first, last, arr, sem):
    xs, ys = first.shape[0] // 96, 64
    per = 8 * CHUNK
    load = pltpu.make_async_copy(arr_hbm, arr, sem.at[0])
    load.start()

    def clear(g, carry):
        tot[pl.ds(pl.multiple_of(g * 8, 8), 8), :] = jnp.zeros((8, LANES), F32)
        return carry

    lax.fori_loop(0, tot.shape[0] // 8, clear, 0, unroll=16)
    load.wait()

    def step(g, carry):
        base = pl.multiple_of(g * per, 8)
        for k in range(64):
            b = names[g * 64 + k]
            row = (b >> 3) * COLUMN + (b & 7) * 4
            at = pl.ds(row, 4)
            tot[at, :] = tot[at, :] + arr[pl.ds(base + (k // 8) * CHUNK + (k % 8) * 4, 4), :]
        return carry

    lax.fori_loop(0, arr.shape[0] // per, step, 0)
    for x in range(xs):
        for r in range(3):
            first[pl.ds(x * 96 + r * 32, 32), :] = tot[pl.ds((x * ys + r) * COLUMN, 32), :]
            last[pl.ds(x * 96 + r * 32, 32), :] = tot[pl.ds((x * ys + ys - 3 + r) * COLUMN, 32), :]


def scatter(arr, names, xs, ys):
    rows = xs * ys * COLUMN + 8
    halo = jax.ShapeDtypeStruct((xs * 96, LANES), F32)
    return call(
        scatter_kernel,
        [hbm(), smem()],
        [vmem()] * 3,
        [jax.ShapeDtypeStruct((rows, LANES), F32), halo, halo],
        [pltpu.VMEM(arr.shape, F32), pltpu.SemaphoreType.DMA((1,))],
    )(arr, names)
ROWS = 72
FACE_X, FACE_Y, FACE_Z, LIQUID = 1, 2, 4, 8
STEP = 0.15


def strip(z):
    return pl.ds(z * LANES, LANES)


def lanes():
    return lax.broadcasted_iota(I32, (ROWS, LANES), 1)


def before_y(a):
    return pltpu.roll(a, 1, 0)


def after_y(a):
    return pltpu.roll(a, ROWS - 1, 0)


def before_z(strips):
    lane = lanes()
    rolled = [pltpu.roll(a, 1, 1) for a in strips]
    return [jnp.where(lane == 0, rolled[z - 1], rolled[z]) for z in range(len(strips))]


def after_z(strips):
    lane = lanes()
    rolled = [pltpu.roll(a, LANES - 1, 1) for a in strips]
    last = len(strips) - 1
    return [jnp.where(lane == LANES - 1, rolled[z + 1 if z < last else 0], rolled[z]) for z in range(len(strips))]


def strips_of(ref, index, count):
    return [ref[(*index, slice(None), strip(z))] for z in range(count)]


def code_kernel(flags, tile, beyond, code):
    xs, zs = code.shape[0], code.shape[2] // LANES

    def encoded(x):
        def one(z):
            f = flags[x, :, strip(z)]
            return jnp.concatenate([jnp.where(f == 2, 0, f + 1), tile[x, :, strip(z)]], 0)

        return [one(z) for z in range(zs)]

    def layer(x, e, e_next):
        o = [jnp.minimum(a, 1) for a in e]
        o_z = after_z(o)
        lane = lanes()
        o_z[-1] = jnp.where(lane == LANES - 1, 0, o_z[-1])
        for z in range(zs):
            c = o[z] & jnp.minimum(e_next[z], 1)
            c = c | ((o[z] & after_y(o[z])) << 1) | ((o[z] & o_z[z]) << 2)
            code[x, :, strip(z)] = c | jnp.where(e[z] == 2, LIQUID, 0)

    def step(x, carry):
        layer(x, encoded(x), encoded(x + 1))
        return carry

    lax.fori_loop(0, xs - 1, step, 0)
    layer(xs - 1, encoded(xs - 1), strips_of(beyond, (), zs))


def make_code(flags, tile, beyond):
    xs, _, nz = flags.shape
    return call(
        code_kernel, [vmem()] * 3, vmem(), jax.ShapeDtypeStruct((xs, ROWS, nz), I32)
    )(flags, tile, beyond)


def partial_spread(v, x, zs):
    vx, vy, vz = (strips_of(v, (a, x), zs) for a in range(3))
    vz_before = before_z(vz)
    return [vx[z] + (vy[z] - before_y(vy[z])) + (vz[z] - vz_before[z]) for z in range(zs)]


def send_layers(v, to_next, to_prior, xs, zs):
    for z, s in enumerate(partial_spread(v, 0, zs)):
        to_prior[:, strip(z)] = s
    to_next[...] = v[0, xs - 1]


def fill(read, code, guess, inverse, v, x, rows, z):
    at = (x, rows, strip(z))
    r = 1.0 / (read(3) + 1.0)
    inverse[at] = r
    bits = code[at]
    for a in range(3):
        g = read(a) * r
        guess[(a, *at)] = g
        v[(a, *at)] = jnp.where(bits & (1 << a) != 0, g, 0.0)


def fields_kernel(tot, code, guess, inverse, v):
    xs, ys, zs = code.shape[0], ROWS - 8, code.shape[2] // LANES

    def step(x, carry):
        for z in range(zs):
            for y in range(0, ys, 8):
                start = (x * ys + y) * COLUMN + z * 4
                read = lambda c: tot[pl.ds(start + c, 8, stride=COLUMN), :]
                fill(read, code, guess, inverse, v, x, slice(y, y + 8), z)
        return carry

    lax.fori_loop(0, xs, step, 0)


def fields(tot, code):
    xs, _, nz = code.shape
    one = jax.ShapeDtypeStruct((xs, ROWS, nz), F32)
    three = jax.ShapeDtypeStruct((3, xs, ROWS, nz), F32)
    return call(fields_kernel, [vmem()] * 2, [vmem()] * 3, [three, one, three])(tot, code)


def edge_kernel(after, prior, code, guess_in, inverse_in, v_in, guess, inverse, v, to_next, to_prior, edge):
    xs, ys, zs = code.shape[0], ROWS - 8, code.shape[2] // LANES
    for x in range(xs):
        edge[pl.ds(x * 256, 96), :] = after[pl.ds(x * 96, 96), :]
        edge[pl.ds(x * 256 + 96, 64), :] = jnp.zeros((64, LANES), F32)
        edge[pl.ds(x * 256 + 160, 96), :] = prior[pl.ds(x * 96, 96), :]

    def step(x, carry):
        for z in range(zs):
            read = lambda c: edge[pl.ds(x * 256 + z * 4 + c, 8, stride=32), :]
            fill(read, code, guess, inverse, v, x, slice(ys, ROWS), z)
        return carry

    lax.fori_loop(0, xs, step, 0)
    send_layers(v, to_next, to_prior, xs, zs)


def add_edge(after, prior, code, guess, inverse, v):
    xs, _, nz = code.shape
    layer = jax.ShapeDtypeStruct((ROWS, nz), F32)
    shapes = [jax.ShapeDtypeStruct(a.shape, F32) for a in (guess, inverse, v)]
    return call(
        edge_kernel,
        [vmem()] * 6,
        [vmem()] * 5,
        shapes + [layer, layer],
        [pltpu.VMEM((xs * 256, LANES), F32)],
        limit=4,
        micros=1,
        input_output_aliases={3: 0, 4: 1, 5: 2},
    )(after, prior, code, guess, inverse, v)


def ascend(p_out, p_in, v, code, x, before, first, zs):
    spread = partial_spread(v, x, zs)
    for z in range(zs):
        s = spread[z] - before(z)
        old = -STEP * s if first else p_in[x, :, strip(z)] - STEP * s
        liquid = code[x, :, strip(z)] & LIQUID != 0
        p_out[x, :, strip(z)] = jnp.where(liquid, jnp.maximum(old, 0.0), 0.0)


def push(v_out, p, code, guess, inverse, x, after, zs):
    here = strips_of(p, (x,), zs)
    here_z = after_z(here)
    for z in range(zs):
        r = inverse[x, :, strip(z)]
        bits = code[x, :, strip(z)]
        beyond = (after(z), after_y(here[z]), here_z[z])
        for a in range(3):
            moved = guess[a, x, :, strip(z)] + (here[z] - beyond[a]) * r
            v_out[a, x, :, strip(z)] = jnp.where(bits & (1 << a) != 0, moved, 0.0)


def climb_inside(first, p_in, v_in, code, guess, inverse, p, v):
    xs, zs = code.shape[0], code.shape[2] // LANES

    def up(x, carry):
        ascend(p, p_in, v_in, code, x, lambda z: v_in[0, x - 1, :, strip(z)], first, zs)
        return carry

    lax.fori_loop(1, xs, up, 0)

    def out(x, carry):
        push(v, p, code, guess, inverse, x, lambda z: p[x + 1, :, strip(z)], zs)
        return carry

    lax.fori_loop(1, xs - 1, out, 0)


def climb_outside(first, before, spread, beyond, p8_in, p_in, v_in, code, guess, inverse, p, v, p8):
    xs, zs = code.shape[0], code.shape[2] // LANES
    ascend(p, p_in, v_in, code, 0, lambda z: before[:, strip(z)], first, zs)
    for z in range(zs):
        s = spread[:, strip(z)] - v_in[0, xs - 1, :, strip(z)]
        old = -STEP * s if first else p8_in[:, strip(z)] - STEP * s
        p8[:, strip(z)] = jnp.where(beyond[:, strip(z)] == 2, jnp.maximum(old, 0.0), 0.0)
    push(v, p, code, guess, inverse, 0, lambda z: p[1, :, strip(z)], zs)
    push(v, p, code, guess, inverse, xs - 1, lambda z: p8[:, strip(z)], zs)


def turn(v, guess, change, x):
    ys, zs = ROWS - 8, v.shape[3] // LANES
    for a in range(3):
        for z in range(zs):
            for y in range(0, ys, 8):
                at = (a, x, slice(y, y + 8), strip(z))
                change[pl.ds((x * ys + y) * COLUMN + z * 4 + a, 8, stride=COLUMN), :] = v[at] - guess[at]


def inner_first_kernel(v_in, code, guess, inverse, p, v):
    climb_inside(True, None, v_in, code, guess, inverse, p, v)


def inner_kernel(p_in, v_in, code, guess, inverse, p, v):
    climb_inside(False, p_in, v_in, code, guess, inverse, p, v)


def layer_copies(p, v, p_out, v_out, x, sem):
    ys = ROWS - 8
    rows = pl.ds(0, ys)
    yield pltpu.make_async_copy(p.at[x, rows], p_out.at[x], sem)
    for a in range(3):
        yield pltpu.make_async_copy(v.at[a, x, rows], v_out.at[a, x], sem)


def inner_last_kernel(p_in, v_in, code, guess, inverse, p, v, change, p_out, v_out, sem):
    climb_inside(False, p_in, v_in, code, guess, inverse, p, v)
    xs = code.shape[0]

    def step(x, carry):
        for copy in layer_copies(p, v, p_out, v_out, x, sem.at[x]):
            copy.start()
        turn(v, guess, change, x)
        return carry

    lax.fori_loop(1, xs - 1, step, 0)
    for x in range(1, xs - 1):
        for copy in layer_copies(p, v, p_out, v_out, x, sem.at[x]):
            copy.wait()


def outer_first_kernel(before, spread, beyond, p_in, v_in, code, guess, inverse, p, v, p8, to_next, to_prior):
    climb_outside(True, before, spread, beyond, None, p_in, v_in, code, guess, inverse, p, v, p8)
    send_layers(v, to_next, to_prior, code.shape[0], code.shape[2] // LANES)


def outer_kernel(before, spread, beyond, p8_in, p_in, v_in, code, guess, inverse, p, v, p8, to_next, to_prior):
    climb_outside(False, before, spread, beyond, p8_in, p_in, v_in, code, guess, inverse, p, v, p8)
    send_layers(v, to_next, to_prior, code.shape[0], code.shape[2] // LANES)


def outer_last_kernel(
    before, spread, beyond, p8_in, names, change_in, p_in, v_in, code, guess, inverse, p_out_in, v_out_in,
    p, v, change, p_out, v_out, reply_out, p8, reply, sem, reply_sem
):
    climb_outside(False, before, spread, beyond, p8_in, p_in, v_in, code, guess, inverse, p, v, p8)
    ends = (0, code.shape[0] - 1)
    for i, x in enumerate(ends):
        for copy in layer_copies(p, v, p_out, v_out, x, sem.at[i]):
            copy.start()
    for x in ends:
        turn(v, guess, change, x)
    steps = reply.shape[0] // 192

    def piece(g):
        rows = pl.ds(pl.multiple_of(g * 192, 192), 192)
        return pltpu.make_async_copy(reply.at[rows], reply_out.at[rows], reply_sem.at[g])

    def step(g, carry):
        base = pl.multiple_of(g * 192, 192)
        for k in range(64):
            b = names[g * 64 + k]
            reply[pl.ds(base + 3 * k, 3), :] = change[pl.ds((b >> 3) * COLUMN + (b & 7) * 4, 3), :]
        piece(g).start()
        return carry

    lax.fori_loop(0, steps, step, 0)

    def finish(g, carry):
        piece(g).wait()
        return carry

    lax.fori_loop(0, steps, finish, 0)
    for i, x in enumerate(ends):
        for copy in layer_copies(p, v, p_out, v_out, x, sem.at[i]):
            copy.wait()


def like(*arrays):
    return [jax.ShapeDtypeStruct(a.shape, F32) for a in arrays]


def climb(names, v, code, guess, inverse, beyond, to_next, to_prior):
    xs, _, nz = code.shape
    rows = xs * (ROWS - 8) * COLUMN + 8
    for sweep in range(ITERS):
        before = shifted(to_next, "slab", 1)
        spread = shifted(to_prior, "slab", -1)
        rest = (code, guess, inverse)
        if sweep == 0:
            p, v = call(
                inner_first_kernel, [vmem()] * 4, [vmem()] * 2, like(inverse, v), input_output_aliases={0: 1}
            )(v, *rest)
            p, v, p8, to_next, to_prior = call(
                outer_first_kernel,
                [vmem()] * 8,
                [vmem()] * 5,
                like(p, v, before, before, before),
                micros=1,
                input_output_aliases={3: 0, 4: 1},
            )(before, spread, beyond, p, v, *rest)
        elif sweep < ITERS - 1:
            p, v = call(
                inner_kernel, [vmem()] * 5, [vmem()] * 2, like(p, v), input_output_aliases={0: 0, 1: 1}
            )(p, v, *rest)
            p, v, p8, to_next, to_prior = call(
                outer_kernel,
                [vmem()] * 9,
                [vmem()] * 5,
                like(p, v, before, before, before),
                micros=1,
                input_output_aliases={4: 0, 5: 1},
            )(before, spread, beyond, p8, p, v, *rest)
        else:
            change = jax.ShapeDtypeStruct((rows, LANES), F32)
            p_out = jax.ShapeDtypeStruct((xs, ROWS - 8, nz), F32)
            v_out = jax.ShapeDtypeStruct((3, xs, ROWS - 8, nz), F32)
            p, v, change, p_out, v_out = call(
                inner_last_kernel,
                [vmem()] * 5,
                [vmem()] * 3 + [hbm()] * 2,
                like(p, v) + [change, p_out, v_out],
                [pltpu.SemaphoreType.DMA((xs,))],
                micros=5,
                input_output_aliases={0: 0, 1: 1},
            )(p, v, *rest)
            reply = jax.ShapeDtypeStruct((names.shape[0] * 3, LANES), F32)
            p, v, change, p_out, v_out, reply = call(
                outer_last_kernel,
                [vmem()] * 4 + [smem()] + [vmem()] * 6 + [hbm()] * 2,
                [vmem()] * 3 + [hbm()] * 3,
                like(p, v, change, p_out, v_out) + [reply],
                [
                    pltpu.VMEM(before.shape, F32),
                    pltpu.VMEM(reply.shape, F32),
                    pltpu.SemaphoreType.DMA((2,)),
                    pltpu.SemaphoreType.DMA((reply.shape[0] // 192,)),
                ],
                input_output_aliases={5: 2, 6: 0, 7: 1, 11: 3, 12: 4},
            )(before, spread, beyond, p8, names, change, p, v, *rest, p_out, v_out)
    return p_out, v_out, reply


def shifted(block, axis, distance):
    devices = range(lax.axis_size(axis))
    return lax.ppermute(block, axis, [(i - distance, i) for i in devices if i - distance in devices])


ITERS = 3


def on_device(velocity, weight, offset, owner, brick, flags):
    devices = lax.axis_size("slab") * lax.axis_size("sub")
    xs, ys, nz = flags.shape
    both = ("slab", "sub")
    kinds = jnp.where(flags == 2, 0, flags + 1)
    later = shifted(kinds[:, :4], "sub", -1)
    prior = shifted(kinds[:, ys - 3 :], "sub", 1)
    tile = jnp.concatenate([later, jnp.zeros((xs, 1, nz), I32), prior], 1)
    beyond = shifted(jnp.concatenate([kinds[0], tile[0]], 0), "slab", -1)
    planes = velocity.transpose(1, 0, 2)
    outgoing, place = splat(planes, weight, offset, owner[:, 0], brick[:, 0], devices)
    arrived = lax.all_to_all(outgoing.reshape(devices, 1, CHUNK * LANES), both, 0, 0, tiled=True)
    code = make_code(flags, tile, beyond)
    arrived, code, beyond = lax.optimization_barrier((arrived, code, beyond))
    names = arrived[:, 0, 32 * LANES : 32 * LANES + 8].astype(I32).reshape(-1)
    totals, first_rows, last_rows = scatter(arrived.reshape(devices * CHUNK, LANES), names, xs, ys)
    after = shifted(first_rows, "sub", -1)
    before = shifted(last_rows, "sub", 1)
    guess, inverse, v = fields(totals, code)
    guess, inverse, v, to_next, to_prior = add_edge(after, before, code, guess, inverse, v)
    p, v, reply = climb(names, v, code, guess, inverse, beyond, to_next, to_prior)
    back = lax.all_to_all(reply.reshape(devices, 24, LANES), both, 0, 0, tiled=True)
    updated = pick(back.reshape(devices * 24, LANES), planes, offset, place)
    return updated.transpose(1, 0, 2), p, v


def solution(mesh):
    return jax.shard_map(
        on_device,
        mesh=mesh,
        in_specs=(P(("slab", "sub")),) * 5 + (P("slab", "sub"),),
        out_specs=(P(("slab", "sub")), P("slab", "sub"), P(None, "slab", "sub")),
        check_vma=False,
    )
```

time: 201 us -> 170 us (0.85)
  blocking collectives: 0 us -> 41.5 us
  waiting for transfers between devices: 61.3 us -> 35.1 us
  local copies, waits for them, and re-layouts: 23 us -> 0.27 us
  Pallas kernels: 61.3 us -> 47 us
  starting transfers between devices: 50.1 us -> 43.1 us
    all_to_all x0 -> x1, blocking collectives: none -> 41.5 us  [on_device(): lax.all_to_all(reply.reshape(devices, 24, LANES), both, 0, 0, tiled=True)]
    all_to_all x1 -> x0, waiting for transfers between devices: 16.5 us -> none  [on_device(): lax.all_to_all(reply.reshape(devices, 24, LANES), both, 0, 0, tiled=True)]
    unnamed x26 -> x10, local copies, waits for them, and re-layouts: 13.7 us -> 0.03 us
    all_to_all x1 -> x0, starting transfers between devices: 10.6 us -> none  [on_device(): lax.all_to_all(reply.reshape(devices, 24, LANES), both, 0, 0, tiled=True)]
    pallas_call x1, Pallas kernels: 15.3 us -> 5.55 us  [pick(): call(pick_kernel, [vmem()] * 3 + [smem()], vmem(), jax.ShapeDtypeStruct((...]
    slice x2 -> x0, local copies, waits for them, and re-layouts: 8.08 us -> none  [on_device(): return (updated.transpose(1, 0, 2), p[:, :ys], v[:, :, :ys])]
    ppermute x11, waiting for transfers between devices: 40.3 us -> 35.1 us  [shifted(): lax.ppermute(block, axis, [(i - distance, i) for i in devices if i - dist...]
    all_to_all x1, waiting for transfers between devices: 4.54 us -> 0.01 us  [on_device(): lax.all_to_all(outgoing.reshape(devices, 1, CHUNK * LANES), both, 0, 0, t...]
  transfers between devices with their start and end apart: 13 -> 12, of which waited for: 10 -> 8; matrix products, arithmetic and copies ran while one was open for 6% -> 0% of each run, Pallas kernels for 5% -> 10%
where the time goes in v1:
time: 170 us; the launch traced here: 169 us
  Pallas kernels  47 us (28%)
  starting transfers between devices  43.1 us (25%)
  blocking collectives  41.5 us (24%)
  waiting for transfers between devices  35.1 us (21%)
    all_to_all x1, blocking collectives, on_device(): lax.all_to_all(reply.reshape(devices, 24, LANES), both, 0, 0, tiled=True)  41.5 us
    ppermute x11, waiting for transfers between devices, shifted(): lax.ppermute(block, axis, [(i - distance, i) for i in devices if i - dist...  35.1 us
    ppermute x11, starting transfers between devices, shifted(): lax.ppermute(block, axis, [(i - distance, i) for i in devices if i - dist...  31.2 us
    all_to_all x1, starting transfers between devices, on_device(): lax.all_to_all(outgoing.reshape(devices, 1, CHUNK * LANES), both, 0, 0, t...  11.9 us
    pallas_call x1, Pallas kernels, splat(): call(splat_kernel, [hbm()] * 5, [vmem(), smem()], [jax.ShapeDtypeStruct((...  9.15 us
    pallas_call x1, Pallas kernels, scatter(): call(scatter_kernel, [hbm(), smem()], [vmem()] * 3, [jax.ShapeDtypeStruct...  7.05 us
    pallas_call x1, Pallas kernels, climb(): call(outer_last_kernel, [vmem()] * 4 + [smem()] + [vmem()] * 6 + [hbm()]...  6.16 us
    pallas_call x1, Pallas kernels, climb(): call(inner_last_kernel, [vmem()] * 5, [vmem()] * 3 + [hbm()] * 2, like(p,...  5.99 us
  transfers between devices with their start and end apart: 12, of which 8 were waited for; matrix products, arithmetic and copies ran while one was open for 0% of the time, Pallas kernels for 10%

profile of v1, /device:TPU:1, one launch (start us, length us, event | category | flops | bytes accessed | tf_op | source)
XLA Modules:
  0.0 169.3 jit_solution(602995761652417894)
XLA Ops:
  0.6 9.2 %shard_map.85 = (f32[4224,128]{1,0:T(8,128)}, s32[512]{0:T(512)}) custom-call(f32[3,512,128]{2,1,0:T(8,128)} %bitcast.15, f32[512,128]{1,0:T(8,128)} %weight_hbm.1, s32[512,128]{1,0:T(8,128)} %offset.1, s32[512]{0:T(512)} %bitcast.19, s32[512]{0:T(512)} %bitcast.20), custom_call_target="tpu_custom_call" | custom-call | flops 800000000 | bytes 1048576 | tf_op jit(solution)/shard_map/pallas_call | solution.py:127
  9.8 11.9 %all-to-all-start = ((f32[128,1,4224]{2,1,0:T(1,128)}), f32[128,1,4224]{2,1,0:T(1,128)}, u32[]{:S(2)}, u32[]{:S(2)}) async-start(f32[128,1,4224]{2,1,0:T(1,128)} %bitcast.17), calls=%async_computation | async-start | bytes 4325376 | tf_op jit(solution)/shard_map/all_to_all | solution.py:615
  22.0 3.2 %collective-permute-start = (s32[8,4,1024]{2,1,0:T(4,128)S(1)}, s32[8,4,1024]{2,1,0:T(4,128)S(1)}, u32[]{:S(2)}, u32[]{:S(2)}) collective-permute-start(s32[8,4,1024]{2,1,0:T(4,128)S(1)} %slice.20), channel_id=1, source_target_pairs={{1,0},{2,1},{3,2},{4,3},{5,4},{6,5},{7,6},{9,8},{10,9},{11,10},{12... | collective-permute-start | bytes 393224 | tf_op jit(solution)/shard_map/ppermute | solution.py:598
  25.2 2.5 %collective-permute-start.1 = (s32[8,3,1024]{2,1,0:T(4,128)S(1)}, s32[8,3,1024]{2,1,0:T(4,128)S(1)}, u32[]{:S(2)}, u32[]{:S(2)}) collective-permute-start(s32[8,3,1024]{2,1,0:T(4,128)S(1)} %slice.21), channel_id=1, source_target_pairs={{0,1},{1,2},{2,3},{3,4},{4,5},{5,6},{6,7},{8,9},{9,10},{10,11},{11... | collective-permute-start | bytes 294920 | tf_op jit(solution)/shard_map/ppermute | solution.py:598
  27.9 17.9 %collective-permute-done.1 = s32[8,3,1024]{2,1,0:T(4,128)S(1)} collective-permute-done((s32[8,3,1024]{2,1,0:T(4,128)S(1)}, s32[8,3,1024]{2,1,0:T(4,128)S(1)}, u32[]{:S(2)}, u32[]{:S(2)}) %collective-permute-start.1) | collective-permute-done | bytes 98336 | tf_op jit(solution)/shard_map/ppermute | solution.py:598
  45.7 2.2 %collective-permute-done = s32[8,4,1024]{2,1,0:T(4,128)S(1)} collective-permute-done((s32[8,4,1024]{2,1,0:T(4,128)S(1)}, s32[8,4,1024]{2,1,0:T(4,128)S(1)}, u32[]{:S(2)}, u32[]{:S(2)}) %collective-permute-start) | collective-permute-done | bytes 131104 | tf_op jit(solution)/shard_map/ppermute | solution.py:598
  48.1 1.3 collective-permute-start.2
  49.4 6.2 %collective-permute-done.2.beyond = s32[72,1024]{1,0:T(8,128)S(1)} collective-permute-done((s32[72,1024]{1,0:T(8,128)S(1)}, s32[72,1024]{1,0:T(8,128)S(1)}, u32[]{:S(2)}, u32[]{:S(2)}) %collective-permute-start.2) | collective-permute-done | bytes 294944 | tf_op jit(solution)/shard_map/ppermute | solution.py:598
  55.5 1.9 %shard_map.86.code = s32[8,72,1024]{2,1,0:T(8,128)S(1)} custom-call(s32[8,64,1024]{2,1,0:T(8,128)S(1)} %copy-done.1, s32[8,8,1024]{2,1,0:T(8,128)S(1)} %pad_add_fusion.1.tile, s32[72,1024]{1,0:T(8,128)S(1)} %collective-permute-done.2.beyond), custom_call_target="tpu_custom_call" | custom-call | flops 300000000 | bytes 1048576 | tf_op jit(solution)/shard_map/pallas_call | solution.py:313
  57.4 1.0 convert_reduce_fusion
  58.5 7.0 %shard_map.87 = (f32[16904,128]{1,0:T(8,128)S(1)}, f32[768,128]{1,0:T(8,128)S(1)}, f32[768,128]{1,0:T(8,128)S(1)}) custom-call(f32[4224,128]{1,0:T(8,128)} %bitcast.6.arr_hbm, s32[1024]{0:T(1024)S(1)} %convert_element_type.8.names), custom_call_target="tpu_custom_call" | custom-call | flops 300000000 | bytes 1048576 | tf_op jit(solution)/shard_map/pallas_call | solution.py:238
  65.6 1.9 %collective-permute-start.3 = (f32[768,128]{1,0:T(8,128)S(1)}, f32[768,128]{1,0:T(8,128)S(1)}, u32[]{:S(2)}, u32[]{:S(2)}) collective-permute-start(f32[768,128]{1,0:T(8,128)S(1)} %get-tuple-element.43), channel_id=1, source_target_pairs={{1,0},{2,1},{3,2},{4,3},{5,4},{6,5},{7,6},{9,8},{10,9},{11,10},{12... | collective-permute-start | bytes 1179656 | tf_op jit(solution)/shard_map/ppermute | solution.py:598
  67.5 6.2 %collective-permute-start.4 = (f32[768,128]{1,0:T(8,128)S(1)}, f32[768,128]{1,0:T(8,128)S(1)}, u32[]{:S(2)}, u32[]{:S(2)}) collective-permute-start(f32[768,128]{1,0:T(8,128)S(1)} %get-tuple-element.44), channel_id=1, source_target_pairs={{0,1},{1,2},{2,3},{3,4},{4,5},{5,6},{6,7},{8,9},{9,10},{10,11},{11... | collective-permute-start | bytes 1179656 | tf_op jit(solution)/shard_map/ppermute | solution.py:598
  73.7 1.9 %shard_map.88 = (f32[3,8,72,1024]{3,2,1,0:T(8,128)S(1)}, f32[8,72,1024]{2,1,0:T(8,128)S(1)}, f32[3,8,72,1024]{3,2,1,0:T(8,128)S(1)}) custom-call(f32[16904,128]{1,0:T(8,128)S(1)} %get-tuple-element.46.tot, s32[8,72,1024]{2,1,0:T(8,128)S(1)} %shard_map.86.code), custom_call_target="tpu_custom_call" | custom-call | flops 300000000 | bytes 1048576 | tf_op jit(solution)/shard_map/pallas_call | solution.py:359
  75.6 1.6 collective-permute-done.3.after
  77.2 1.2 collective-permute-done.4.prior
  79.4 3.5 %collective-permute-start.5 = (f32[72,1024]{1,0:T(8,128)S(1)}, f32[72,1024]{1,0:T(8,128)S(1)}, u32[]{:S(2)}, u32[]{:S(2)}) collective-permute-start(f32[72,1024]{1,0:T(8,128)S(1)} %get-tuple-element.50), channel_id=1, source_target_pairs={{0,8},{8,16},{16,24},{24,32},{32,40},{40,48},{48,56},{56,64},{64,7... | collective-permute-start | bytes 884744 | tf_op jit(solution)/shard_map/ppermute | solution.py:598
  82.9 1.3 collective-permute-start.6
  84.2 3.1 %shard_map.90 = (f32[8,72,1024]{2,1,0:T(8,128)S(1)}, f32[3,8,72,1024]{3,2,1,0:T(8,128)S(1)}) custom-call(f32[3,8,72,1024]{3,2,1,0:T(8,128)S(1)} %get-tuple-element.53.v_in, s32[8,72,1024]{2,1,0:T(8,128)S(1)} %shard_map.86.code, f32[3,8,72,1024]{3,2,1,0:T(8,128)S(1)} %get-tuple-element.54.guess, ...), custom_call_target="tpu_custom_call", output_to_operand_aliasing={{1}: (0, {})} | custom-call | flops 300000000 | bytes 1048576 | tf_op jit(solution)/shard_map/pallas_call | solution.py:543
  87.3 3.1 %collective-permute-done.6.spread = f32[72,1024]{1,0:T(8,128)S(1)} collective-permute-done((f32[72,1024]{1,0:T(8,128)S(1)}, f32[72,1024]{1,0:T(8,128)S(1)}, u32[]{:S(2)}, u32[]{:S(2)}) %collective-permute-start.6) | collective-permute-done | bytes 294944 | tf_op jit(solution)/shard_map/ppermute | solution.py:598
  90.3 1.0 shard_map.91
  91.3 5.0 %collective-permute-start.7 = (f32[72,1024]{1,0:T(8,128)S(1)}, f32[72,1024]{1,0:T(8,128)S(1)}, u32[]{:S(2)}, u32[]{:S(2)}) collective-permute-start(f32[72,1024]{1,0:T(8,128)S(1)} %get-tuple-element.58), channel_id=1, source_target_pairs={{0,8},{8,16},{16,24},{24,32},{32,40},{40,48},{48,56},{56,64},{64,7... | collective-permute-start | bytes 884744 | tf_op jit(solution)/shard_map/ppermute | solution.py:598
  96.3 1.3 collective-permute-start.8
  97.6 3.3 %shard_map.92 = (f32[8,72,1024]{2,1,0:T(8,128)S(1)}, f32[3,8,72,1024]{3,2,1,0:T(8,128)S(1)}) custom-call(f32[8,72,1024]{2,1,0:T(8,128)S(1)} %get-tuple-element.61.p_in, f32[3,8,72,1024]{3,2,1,0:T(8,128)S(1)} %get-tuple-element.62.v_in, s32[8,72,1024]{2,1,0:T(8,128)S(1)} %shard_map.86.code, ...), custom_call_target="tpu_custom_call", output_to_operand_aliasing={{0}: (0, {}), {1}: (1, {})} | custom-call | flops 300000000 | bytes 1048576 | tf_op jit(solution)/shard_map/pallas_call | solution.py:555
  100.9 2.9 %collective-permute-done.8.spread = f32[72,1024]{1,0:T(8,128)S(1)} collective-permute-done((f32[72,1024]{1,0:T(8,128)S(1)}, f32[72,1024]{1,0:T(8,128)S(1)}, u32[]{:S(2)}, u32[]{:S(2)}) %collective-permute-start.8) | collective-permute-done | bytes 294944 | tf_op jit(solution)/shard_map/ppermute | solution.py:598
  103.8 1.0 shard_map.93
  104.8 3.7 %collective-permute-start.9 = (f32[72,1024]{1,0:T(8,128)S(1)}, f32[72,1024]{1,0:T(8,128)S(1)}, u32[]{:S(2)}, u32[]{:S(2)}) collective-permute-start(f32[72,1024]{1,0:T(8,128)S(1)} %get-tuple-element.65), channel_id=1, source_target_pairs={{0,8},{8,16},{16,24},{24,32},{32,40},{40,48},{48,56},{56,64},{64,7... | collective-permute-start | bytes 884744 | tf_op jit(solution)/shard_map/ppermute | solution.py:598
  108.6 1.3 collective-permute-start.10
  109.9 6.0 %shard_map.94 = (f32[8,72,1024]{2,1,0:T(8,128)S(1)}, f32[3,8,72,1024]{3,2,1,0:T(8,128)S(1)}, f32[16904,128]{1,0:T(8,128)S(1)}, f32[8,64,1024]{2,1,0:T(8,128)}, f32[3,8,64,1024]{3,2,1,0:T(8,128)}) custom-call(f32[8,72,1024]{2,1,0:T(8,128)S(1)} %get-tuple-element.68.p_in, ...), custom_call_target="tpu_custom_call", output_to_operand_aliasing={{0}: (0, {}), {1}: (1, {})} | custom-call | flops 500000000 | bytes 1048576 | tf_op jit(solution)/shard_map/pallas_call | solution.py:570
  116.0 6.2 %shard_map.95 = (f32[8,72,1024]{2,1,0:T(8,128)S(1)}, f32[3,8,72,1024]{3,2,1,0:T(8,128)S(1)}, f32[16904,128]{1,0:T(8,128)S(1)}, f32[8,64,1024]{2,1,0:T(8,128)}, f...) custom-call(f32[72,1024]{1,0:T(8,128)S(1)} %collective-permute-done., ...), custom_call_target="tpu_custom_call", output_to_operand_aliasing={{2}: (5, {}), {0}: (6, {}), {1}: (7, {}), {3}: (11, {}), {4... | custom-call | flops 300000000 | bytes 1048576 | tf_op jit(solution)/shard_map/pallas_call | solution.py:580
  122.2 41.5 %all_to_all.10 = f32[128,24,128]{2,1,0:T(8,128)S(1)} all-to-all(f32[128,24,128]{2,1,0:T(8,128)S(1)} %bitcast.14), channel_id=1, replica_groups=mesh['slab'=16,'sub'=8] {'slab','sub'}, dimensions={0} | all-to-all | bytes 3145728 | tf_op jit(solution)/shard_map/all_to_all | solution.py:625
  163.8 5.5 %shard_map.96 = f32[3,512,128]{2,1,0:T(8,128)} custom-call(f32[3072,128]{1,0:T(8,128)S(1)} %bitcast.13, f32[3,512,128]{2,1,0:T(8,128)S(1)} %bitcast.16, s32[512,128]{1,0:T(8,128)S(1)} %copy-done.3, s32[512]{0:T(512)S(1)} %copy-done.4), custom_call_target="tpu_custom_call" | custom-call | flops 600000000 | bytes 1048576 | tf_op jit(solution)/shard_map/pallas_call | solution.py:195
  (25 shorter events, 1.7 us)
Async XLA Ops:
  9.8 11.9 %copy-start = (s32[8,64,1024]{2,1,0:T(8,128)S(1)}, s32[8,64,1024]{2,1,0:T(8,128)}, u32[]{:S(2)}) copy-start(s32[8,64,1024]{2,1,0:T(8,128)} %flags.1) | copy-start | bytes 6291460
  9.8 47.6 %all-to-all-start = ((f32[128,1,4224]{2,1,0:T(1,128)}), f32[128,1,4224]{2,1,0:T(1,128)}, u32[]{:S(2)}, u32[]{:S(2)}) async-start(f32[128,1,4224]{2,1,0:T(1,128)} %bitcast.17), calls=%async_computation | async-start | bytes 4325376 | tf_op jit(solution)/shard_map/all_to_all | solution.py:615
  21.7 33.8 %copy-start.1 = (s32[8,64,1024]{2,1,0:T(8,128)S(1)}, s32[8,64,1024]{2,1,0:T(8,128)}, u32[]{:S(2)}) copy-start(s32[8,64,1024]{2,1,0:T(8,128)} %flags.1) | copy-start | bytes 6291460
  22.0 25.9 %collective-permute-start = (s32[8,4,1024]{2,1,0:T(4,128)S(1)}, s32[8,4,1024]{2,1,0:T(4,128)S(1)}, u32[]{:S(2)}, u32[]{:S(2)}) collective-permute-start(s32[8,4,1024]{2,1,0:T(4,128)S(1)} %slice.20), channel_id=1, source_target_pairs={{1,0},{2,1},{3,2},{4,3},{5,4},{6,5},{7,6},{9,8},{10,9},{11,10},{12... | collective-permute-start | bytes 393224 | tf_op jit(solution)/shard_map/ppermute | solution.py:598
  25.2 20.5 %collective-permute-start.1 = (s32[8,3,1024]{2,1,0:T(4,128)S(1)}, s32[8,3,1024]{2,1,0:T(4,128)S(1)}, u32[]{:S(2)}, u32[]{:S(2)}) collective-permute-start(s32[8,3,1024]{2,1,0:T(4,128)S(1)} %slice.21), channel_id=1, source_target_pairs={{0,1},{1,2},{2,3},{3,4},{4,5},{5,6},{6,7},{8,9},{9,10},{10,11},{11... | collective-permute-start | bytes 294920 | tf_op jit(solution)/shard_map/ppermute | solution.py:598
  48.1 7.5 %collective-permute-start.2 = (s32[72,1024]{1,0:T(8,128)S(1)}, s32[72,1024]{1,0:T(8,128)S(1)}, u32[]{:S(2)}, u32[]{:S(2)}) collective-permute-start(s32[72,1024]{1,0:T(8,128)S(1)} %pad_add_fusion), channel_id=1, source_target_pairs={{8,0},{16,8},{24,16},{32,24},{40,32},{48,40},{56,48},{64,56},{72,6... | collective-permute-start | bytes 884744 | tf_op jit(solution)/shard_map/ppermute | solution.py:598
  65.6 11.7 %collective-permute-start.3 = (f32[768,128]{1,0:T(8,128)S(1)}, f32[768,128]{1,0:T(8,128)S(1)}, u32[]{:S(2)}, u32[]{:S(2)}) collective-permute-start(f32[768,128]{1,0:T(8,128)S(1)} %get-tuple-element.43), channel_id=1, source_target_pairs={{1,0},{2,1},{3,2},{4,3},{5,4},{6,5},{7,6},{9,8},{10,9},{11,10},{12... | collective-permute-start | bytes 1179656 | tf_op jit(solution)/shard_map/ppermute | solution.py:598
  67.5 10.9 %collective-permute-start.4 = (f32[768,128]{1,0:T(8,128)S(1)}, f32[768,128]{1,0:T(8,128)S(1)}, u32[]{:S(2)}, u32[]{:S(2)}) collective-permute-start(f32[768,128]{1,0:T(8,128)S(1)} %get-tuple-element.44), channel_id=1, source_target_pairs={{0,1},{1,2},{2,3},{3,4},{4,5},{5,6},{6,7},{8,9},{9,10},{10,11},{11... | collective-permute-start | bytes 1179656 | tf_op jit(solution)/shard_map/ppermute | solution.py:598
  79.4 7.9 %collective-permute-start.5 = (f32[72,1024]{1,0:T(8,128)S(1)}, f32[72,1024]{1,0:T(8,128)S(1)}, u32[]{:S(2)}, u32[]{:S(2)}) collective-permute-start(f32[72,1024]{1,0:T(8,128)S(1)} %get-tuple-element.50), channel_id=1, source_target_pairs={{0,8},{8,16},{16,24},{24,32},{32,40},{40,48},{48,56},{56,64},{64,7... | collective-permute-start | bytes 884744 | tf_op jit(solution)/shard_map/ppermute | solution.py:598
  82.9 7.5 %collective-permute-start.6 = (f32[72,1024]{1,0:T(8,128)S(1)}, f32[72,1024]{1,0:T(8,128)S(1)}, u32[]{:S(2)}, u32[]{:S(2)}) collective-permute-start(f32[72,1024]{1,0:T(8,128)S(1)} %get-tuple-element.51), channel_id=1, source_target_pairs={{8,0},{16,8},{24,16},{32,24},{40,32},{48,40},{56,48},{64,56},{72,6... | collective-permute-start | bytes 884744 | tf_op jit(solution)/shard_map/ppermute | solution.py:598
  91.3 9.6 %collective-permute-start.7 = (f32[72,1024]{1,0:T(8,128)S(1)}, f32[72,1024]{1,0:T(8,128)S(1)}, u32[]{:S(2)}, u32[]{:S(2)}) collective-permute-start(f32[72,1024]{1,0:T(8,128)S(1)} %get-tuple-element.58), channel_id=1, source_target_pairs={{0,8},{8,16},{16,24},{24,32},{32,40},{40,48},{48,56},{56,64},{64,7... | collective-permute-start | bytes 884744 | tf_op jit(solution)/shard_map/ppermute | solution.py:598
  96.3 7.5 %collective-permute-start.8 = (f32[72,1024]{1,0:T(8,128)S(1)}, f32[72,1024]{1,0:T(8,128)S(1)}, u32[]{:S(2)}, u32[]{:S(2)}) collective-permute-start(f32[72,1024]{1,0:T(8,128)S(1)} %get-tuple-element.59), channel_id=1, source_target_pairs={{8,0},{16,8},{24,16},{32,24},{40,32},{48,40},{56,48},{64,56},{72,6... | collective-permute-start | bytes 884744 | tf_op jit(solution)/shard_map/ppermute | solution.py:598
  104.8 11.0 %collective-permute-start.9 = (f32[72,1024]{1,0:T(8,128)S(1)}, f32[72,1024]{1,0:T(8,128)S(1)}, u32[]{:S(2)}, u32[]{:S(2)}) collective-permute-start(f32[72,1024]{1,0:T(8,128)S(1)} %get-tuple-element.65), channel_id=1, source_target_pairs={{0,8},{8,16},{16,24},{24,32},{32,40},{40,48},{48,56},{56,64},{64,7... | collective-permute-start | bytes 884744 | tf_op jit(solution)/shard_map/ppermute | solution.py:598
  108.6 7.5 %collective-permute-start.10 = (f32[72,1024]{1,0:T(8,128)S(1)}, f32[72,1024]{1,0:T(8,128)S(1)}, u32[]{:S(2)}, u32[]{:S(2)}) collective-permute-start(f32[72,1024]{1,0:T(8,128)S(1)} %get-tuple-element.66), channel_id=1, source_target_pairs={{8,0},{16,8},{24,16},{32,24},{40,32},{48,40},{56,48},{64,56},{72,6... | collective-permute-start | bytes 884744 | tf_op jit(solution)/shard_map/ppermute | solution.py:598
  122.2 41.6 %copy-start.2 = (f32[512,3,128]{2,0,1:T(8,128)S(1)}, f32[512,3,128]{2,0,1:T(8,128)}, u32[]{:S(2)}) copy-start(f32[512,3,128]{2,0,1:T(8,128)} %param.6) | copy-start | bytes 2359300
  122.2 41.6 %copy-start.3 = (s32[512,128]{1,0:T(8,128)S(1)}, s32[512,128]{1,0:T(8,128)}, u32[]{:S(2)}) copy-start(s32[512,128]{1,0:T(8,128)} %offset.1) | copy-start | bytes 786436
  122.2 41.6 %copy-start.4 = (s32[512]{0:T(512)S(1)}, s32[512]{0:T(512)}, u32[]{:S(2)}) copy-start(s32[512]{0:T(512)} %get-tuple-element.76.place) | copy-start | bytes 6148

commit v2 on v1

--- a/solution.py
+++ b/solution.py
@@ -1,10 +1,10 @@
-import functools
 import jax
 import jax.numpy as jnp
 from jax import lax
 from jax.experimental import pallas as pl
 from jax.experimental.pallas import tpu as pltpu
 from jax.sharding import PartitionSpec as P
+
 
 F32 = jnp.float32
 BF16 = jnp.bfloat16
@@ -13,7 +13,7 @@
 CHUNK = 33
 COLUMN = 33
 MIB = 1 << 20
-GROUP = 64
+GROUP = 128
 
 
 def vmem():
@@ -218,11 +218,19 @@
 
     def step(g, carry):
         base = pl.multiple_of(g * per, 8)
-        for k in range(64):
-            b = names[g * 64 + k]
-            row = (b >> 3) * COLUMN + (b & 7) * 4
-            at = pl.ds(row, 4)
-            tot[at, :] = tot[at, :] + arr[pl.ds(base + (k // 8) * CHUNK + (k % 8) * 4, 4), :]
+        for first_slot in range(0, 64, 4):
+            slots = range(first_slot, first_slot + 4)
+            rows = []
+            for k in slots:
+                b = names[g * 64 + k]
+                rows.append((b >> 3) * COLUMN + (b & 7) * 4)
+            old = [tot[pl.ds(row, 4), :] for row in rows]
+            new = [arr[pl.ds(base + (k // 8) * CHUNK + (k % 8) * 4, 4), :] for k in slots]
+            for i in range(4):
+                total = old[i] + new[i]
+                for j in range(i):
+                    total = total + jnp.where(rows[j] == rows[i], new[j], 0.0)
+                tot[pl.ds(rows[i], 4), :] = total
         return carry
 
     lax.fori_loop(0, arr.shape[0] // per, step, 0)
@@ -242,8 +250,10 @@
         [jax.ShapeDtypeStruct((rows, LANES), F32), halo, halo],
         [pltpu.VMEM(arr.shape, F32), pltpu.SemaphoreType.DMA((1,))],
     )(arr, names)
+
+
 ROWS = 72
-FACE_X, FACE_Y, FACE_Z, LIQUID = 1, 2, 4, 8
+LIQUID = 8
 STEP = 0.15
 
 
@@ -280,13 +290,46 @@
     return [ref[(*index, slice(None), strip(z))] for z in range(count)]
 
 
+def kind(f):
+    return jnp.where(f == 2, 0, f + 1)
+
+
+def ends_kernel(flags, layer_out, low_out, high_out, layer, low, high, sems):
+    ys = flags.shape[1]
+    copies = [
+        pltpu.make_async_copy(flags.at[0], layer, sems.at[0]),
+        pltpu.make_async_copy(flags.at[:, pl.ds(0, 8)], low, sems.at[1]),
+        pltpu.make_async_copy(flags.at[:, pl.ds(ys - 8, 8)], high, sems.at[2]),
+    ]
+    for copy in copies:
+        copy.start()
+    for copy in copies:
+        copy.wait()
+    layer_out[...] = kind(layer[...])
+    low_out[...] = kind(low[...])[:, :4]
+    high_out[...] = kind(high[...])[:, 4:]
+
+
+def flag_ends(flags):
+    xs, ys, nz = flags.shape
+    layer, rows, few = ((ys, nz), (xs, 8, nz), (xs, 4, nz))
+    return call(
+        ends_kernel,
+        [hbm()],
+        [vmem()] * 3,
+        [jax.ShapeDtypeStruct(a, I32) for a in (layer, few, few)],
+        [pltpu.VMEM(a, I32) for a in (layer, rows, rows)] + [pltpu.SemaphoreType.DMA((3,))],
+        limit=62,
+        micros=1,
+    )(flags)
+
+
 def code_kernel(flags, tile, beyond, code):
     xs, zs = code.shape[0], code.shape[2] // LANES
 
     def encoded(x):
         def one(z):
-            f = flags[x, :, strip(z)]
-            return jnp.concatenate([jnp.where(f == 2, 0, f + 1), tile[x, :, strip(z)]], 0)
+            return jnp.concatenate([kind(flags[x, :, strip(z)]), tile[x, :, strip(z)]], 0)
 
         return [one(z) for z in range(zs)]
 
@@ -401,14 +444,14 @@
         p_out[x, :, strip(z)] = jnp.where(liquid, jnp.maximum(old, 0.0), 0.0)
 
 
-def push(v_out, p, code, guess, inverse, x, after, zs):
+def push(v_out, p, code, guess, inverse, x, after, zs, axes=(0, 1, 2)):
     here = strips_of(p, (x,), zs)
-    here_z = after_z(here)
+    here_z = after_z(here) if 2 in axes else here
     for z in range(zs):
         r = inverse[x, :, strip(z)]
         bits = code[x, :, strip(z)]
-        beyond = (after(z), after_y(here[z]), here_z[z])
-        for a in range(3):
+        beyond = (after(z) if 0 in axes else None, after_y(here[z]), here_z[z])
+        for a in axes:
             moved = guess[a, x, :, strip(z)] + (here[z] - beyond[a]) * r
             v_out[a, x, :, strip(z)] = jnp.where(bits & (1 << a) != 0, moved, 0.0)
 
@@ -427,6 +470,7 @@
         return carry
 
     lax.fori_loop(1, xs - 1, out, 0)
+    push(v, p, code, guess, inverse, xs - 1, None, zs, (1, 2))
 
 
 def climb_outside(first, before, spread, beyond, p8_in, p_in, v_in, code, guess, inverse, p, v, p8):
@@ -437,12 +481,12 @@
         old = -STEP * s if first else p8_in[:, strip(z)] - STEP * s
         p8[:, strip(z)] = jnp.where(beyond[:, strip(z)] == 2, jnp.maximum(old, 0.0), 0.0)
     push(v, p, code, guess, inverse, 0, lambda z: p[1, :, strip(z)], zs)
-    push(v, p, code, guess, inverse, xs - 1, lambda z: p8[:, strip(z)], zs)
-
-
-def turn(v, guess, change, x):
+    push(v, p, code, guess, inverse, xs - 1, lambda z: p8[:, strip(z)], zs, (0,))
+
+
+def turn(v, guess, change, x, axes=(0, 1, 2)):
     ys, zs = ROWS - 8, v.shape[3] // LANES
-    for a in range(3):
+    for a in axes:
         for z in range(zs):
             for y in range(0, ys, 8):
                 at = (a, x, slice(y, y + 8), strip(z))
@@ -457,27 +501,34 @@
     climb_inside(False, p_in, v_in, code, guess, inverse, p, v)
 
 
-def layer_copies(p, v, p_out, v_out, x, sem):
-    ys = ROWS - 8
-    rows = pl.ds(0, ys)
-    yield pltpu.make_async_copy(p.at[x, rows], p_out.at[x], sem)
-    for a in range(3):
-        yield pltpu.make_async_copy(v.at[a, x, rows], v_out.at[a, x], sem)
+def copy_pressure(p, p_out, x, sem):
+    return pltpu.make_async_copy(p.at[x, pl.ds(0, ROWS - 8)], p_out.at[x], sem)
+
+
+def copy_faces(v, v_out, a, x, sem):
+    return pltpu.make_async_copy(v.at[a, x, pl.ds(0, ROWS - 8)], v_out.at[a, x], sem)
 
 
 def inner_last_kernel(p_in, v_in, code, guess, inverse, p, v, change, p_out, v_out, sem):
     climb_inside(False, p_in, v_in, code, guess, inverse, p, v)
     xs = code.shape[0]
 
+    def copies(x, axes):
+        return [copy_pressure(p, p_out, x, sem.at[x])] + [copy_faces(v, v_out, a, x, sem.at[x]) for a in axes]
+
+    for copy in copies(xs - 1, (1, 2)):
+        copy.start()
+
     def step(x, carry):
-        for copy in layer_copies(p, v, p_out, v_out, x, sem.at[x]):
+        for copy in copies(x, (0, 1, 2)):
             copy.start()
         turn(v, guess, change, x)
         return carry
 
     lax.fori_loop(1, xs - 1, step, 0)
-    for x in range(1, xs - 1):
-        for copy in layer_copies(p, v, p_out, v_out, x, sem.at[x]):
+    turn(v, guess, change, xs - 1, (1, 2))
+    for x in range(1, xs):
+        for copy in copies(x, (0, 1, 2) if x < xs - 1 else (1, 2)):
             copy.wait()
 
 
@@ -493,39 +544,28 @@
 
 def outer_last_kernel(
     before, spread, beyond, p8_in, names, change_in, p_in, v_in, code, guess, inverse, p_out_in, v_out_in,
-    p, v, change, p_out, v_out, reply_out, p8, reply, sem, reply_sem
+    p, v, change, p_out, v_out, reply, p8, sem
 ):
     climb_outside(False, before, spread, beyond, p8_in, p_in, v_in, code, guess, inverse, p, v, p8)
-    ends = (0, code.shape[0] - 1)
-    for i, x in enumerate(ends):
-        for copy in layer_copies(p, v, p_out, v_out, x, sem.at[i]):
-            copy.start()
-    for x in ends:
-        turn(v, guess, change, x)
-    steps = reply.shape[0] // 192
-
-    def piece(g):
-        rows = pl.ds(pl.multiple_of(g * 192, 192), 192)
-        return pltpu.make_async_copy(reply.at[rows], reply_out.at[rows], reply_sem.at[g])
+    end = code.shape[0] - 1
+    copies = [copy_pressure(p, p_out, 0, sem.at[0])]
+    copies += [copy_faces(v, v_out, a, 0, sem.at[0]) for a in range(3)]
+    copies.append(copy_faces(v, v_out, 0, end, sem.at[0]))
+    for copy in copies:
+        copy.start()
+    turn(v, guess, change, 0)
+    turn(v, guess, change, end, (0,))
 
     def step(g, carry):
         base = pl.multiple_of(g * 192, 192)
         for k in range(64):
             b = names[g * 64 + k]
             reply[pl.ds(base + 3 * k, 3), :] = change[pl.ds((b >> 3) * COLUMN + (b & 7) * 4, 3), :]
-        piece(g).start()
-        return carry
-
-    lax.fori_loop(0, steps, step, 0)
-
-    def finish(g, carry):
-        piece(g).wait()
-        return carry
-
-    lax.fori_loop(0, steps, finish, 0)
-    for i, x in enumerate(ends):
-        for copy in layer_copies(p, v, p_out, v_out, x, sem.at[i]):
-            copy.wait()
+        return carry
+
+    lax.fori_loop(0, reply.shape[0] // 192, step, 0)
+    for copy in copies:
+        copy.wait()
 
 
 def like(*arrays):
@@ -580,13 +620,11 @@
             p, v, change, p_out, v_out, reply = call(
                 outer_last_kernel,
                 [vmem()] * 4 + [smem()] + [vmem()] * 6 + [hbm()] * 2,
-                [vmem()] * 3 + [hbm()] * 3,
+                [vmem()] * 3 + [hbm()] * 2 + [vmem()],
                 like(p, v, change, p_out, v_out) + [reply],
                 [
                     pltpu.VMEM(before.shape, F32),
-                    pltpu.VMEM(reply.shape, F32),
-                    pltpu.SemaphoreType.DMA((2,)),
-                    pltpu.SemaphoreType.DMA((reply.shape[0] // 192,)),
+                    pltpu.SemaphoreType.DMA((1,)),
                 ],
                 input_output_aliases={5: 2, 6: 0, 7: 1, 11: 3, 12: 4},
             )(before, spread, beyond, p8, names, change, p, v, *rest, p_out, v_out)
@@ -603,15 +641,16 @@
 
 def on_device(velocity, weight, offset, owner, brick, flags):
     devices = lax.axis_size("slab") * lax.axis_size("sub")
-    xs, ys, nz = flags.shape
+    xs, ys, _ = flags.shape
     both = ("slab", "sub")
-    kinds = jnp.where(flags == 2, 0, flags + 1)
-    later = shifted(kinds[:, :4], "sub", -1)
-    prior = shifted(kinds[:, ys - 3 :], "sub", 1)
-    tile = jnp.concatenate([later, jnp.zeros((xs, 1, nz), I32), prior], 1)
-    beyond = shifted(jnp.concatenate([kinds[0], tile[0]], 0), "slab", -1)
+    layer, low, high = flag_ends(flags)
+    beyond_own = shifted(layer, "slab", -1)
+    later = shifted(low, "sub", -1)
+    prior = shifted(high, "sub", 1)
     planes = velocity.transpose(1, 0, 2)
     outgoing, place = splat(planes, weight, offset, owner[:, 0], brick[:, 0], devices)
+    tile = jnp.concatenate([later, prior], 1)
+    beyond = jnp.concatenate([beyond_own, shifted(tile[0], "slab", -1)], 0)
     arrived = lax.all_to_all(outgoing.reshape(devices, 1, CHUNK * LANES), both, 0, 0, tiled=True)
     code = make_code(flags, tile, beyond)
     arrived, code, beyond = lax.optimization_barrier((arrived, code, beyond))

time: 170 us -> 162 us (0.953)
  Pallas kernels: 47 us -> 44.6 us
  starting transfers between devices: 43.1 us -> 40.7 us
  waiting for transfers between devices: 35.1 us -> 32.7 us
  blocking collectives: 41.5 us -> 39.2 us
    pallas_call x1, Pallas kernels: 6.16 us -> 3.62 us  [climb(): call(outer_last_kernel, [vmem()] * 4 + [smem()] + [vmem()] * 6 + [hbm()]...]
    ppermute x11 -> x12, starting transfers between devices: 31.2 us -> 28.8 us  [shifted(): lax.ppermute(block, axis, [(i - distance, i) for i in devices if i - dist...]
    ppermute x11 -> x12, waiting for transfers between devices: 35.1 us -> 32.7 us  [shifted(): lax.ppermute(block, axis, [(i - distance, i) for i in devices if i - dist...]
    all_to_all x1, blocking collectives: 41.5 us -> 39.2 us  [on_device(): lax.all_to_all(reply.reshape(devices, 24, LANES), both, 0, 0, tiled=True)]
    pallas_call x0 -> x1, Pallas kernels: none -> 1.95 us  [flag_ends(): call(ends_kernel, [hbm()], [vmem()] * 3, [jax.ShapeDtypeStruct(a, I32) fo...]
  transfers between devices with their start and end apart: 12 -> 13, of which waited for: 8 -> 8; matrix products, arithmetic and copies ran while one was open for 0% -> 0% of each run, Pallas kernels for 10% -> 12%
where the time goes in v2:
time: 162 us; the launch traced here: 161 us
  Pallas kernels  44.6 us (28%)
  starting transfers between devices  40.7 us (25%)
  blocking collectives  39.2 us (24%)
  waiting for transfers between devices  32.7 us (20%)
  local copies, waits for them, and re-layouts  1.72 us (1%)
    all_to_all x1, blocking collectives, on_device(): lax.all_to_all(reply.reshape(devices, 24, LANES), both, 0, 0, tiled=True)  39.2 us
    ppermute x12, waiting for transfers between devices, shifted(): lax.ppermute(block, axis, [(i - distance, i) for i in devices if i - dist...  32.7 us
    ppermute x12, starting transfers between devices, shifted(): lax.ppermute(block, axis, [(i - distance, i) for i in devices if i - dist...  28.8 us
    all_to_all x1, starting transfers between devices, on_device(): lax.all_to_all(outgoing.reshape(devices, 1, CHUNK * LANES), both, 0, 0, t...  11.9 us
    pallas_call x1, Pallas kernels, splat(): call(splat_kernel, [hbm()] * 5, [vmem(), smem()], [jax.ShapeDtypeStruct((...  8.66 us
    pallas_call x1, Pallas kernels, climb(): call(inner_last_kernel, [vmem()] * 5, [vmem()] * 3 + [hbm()] * 2, like(p,...  6.38 us
    pallas_call x1, Pallas kernels, scatter(): call(scatter_kernel, [hbm(), smem()], [vmem()] * 3, [jax.ShapeDtypeStruct...  5.73 us
    pallas_call x1, Pallas kernels, pick(): call(pick_kernel, [vmem()] * 3 + [smem()], vmem(), jax.ShapeDtypeStruct((...  5.07 us
  transfers between devices with their start and end apart: 13, of which 8 were waited for; matrix products, arithmetic and copies ran while one was open for 0% of the time, Pallas kernels for 12%

profile of v2, /device:TPU:1, one launch (start us, length us, event | category | flops | bytes accessed | tf_op | source)
XLA Modules:
  0.0 160.9 jit_solution(18368752847468728498)
XLA Ops:
  0.6 8.7 %shard_map.85 = (f32[4224,128]{1,0:T(8,128)}, s32[512]{0:T(512)}) custom-call(f32[3,512,128]{2,1,0:T(8,128)} %bitcast.12, f32[512,128]{1,0:T(8,128)} %weight_hbm.1, s32[512,128]{1,0:T(8,128)} %offset.1, s32[512]{0:T(512)} %bitcast.16, s32[512]{0:T(512)} %bitcast.17), custom_call_target="tpu_custom_call" | custom-call | flops 800000000 | bytes 1048576 | tf_op jit(solution)/shard_map/pallas_call | solution.py:127
  9.3 11.9 %all-to-all-start = ((f32[128,1,4224]{2,1,0:T(1,128)}), f32[128,1,4224]{2,1,0:T(1,128)}, u32[]{:S(2)}, u32[]{:S(2)}) async-start(f32[128,1,4224]{2,1,0:T(1,128)} %bitcast.14), calls=%async_computation | async-start | bytes 4325376 | tf_op jit(solution)/shard_map/all_to_all | solution.py:654
  21.2 2.0 %shard_map.86 = (s32[64,1024]{1,0:T(8,128)}, s32[8,4,1024]{2,1,0:T(4,128)}, s32[8,4,1024]{2,1,0:T(4,128)}) custom-call(s32[8,64,1024]{2,1,0:T(8,128)} %flags.3), custom_call_target="tpu_custom_call" | custom-call | flops 100000000 | bytes 1048576 | tf_op jit(solution)/shard_map/pallas_call | solution.py:316
  23.2 3.0 %collective-permute-start = (s32[8,4,1024]{2,1,0:T(4,128)}, s32[8,4,1024]{2,1,0:T(4,128)S(1)}, u32[]{:S(2)}, u32[]{:S(2)}) collective-permute-start(s32[8,4,1024]{2,1,0:T(4,128)} %get-tuple-element.45), channel_id=1, source_target_pairs={{1,0},{2,1},{3,2},{4,3},{5,4},{6,5},{7,6},{9,8},{10,9},{11,10},{12... | collective-permute-start | bytes 393224 | tf_op jit(solution)/shard_map/ppermute | solution.py:636
  26.2 2.5 %collective-permute-start.1 = (s32[8,4,1024]{2,1,0:T(4,128)}, s32[8,4,1024]{2,1,0:T(4,128)S(1)}, u32[]{:S(2)}, u32[]{:S(2)}) collective-permute-start(s32[8,4,1024]{2,1,0:T(4,128)} %get-tuple-element.46), channel_id=1, source_target_pairs={{0,1},{1,2},{2,3},{3,4},{4,5},{5,6},{6,7},{8,9},{9,10},{10,11},{11... | collective-permute-start | bytes 393224 | tf_op jit(solution)/shard_map/ppermute | solution.py:636
  28.7 1.3 collective-permute-start.2
  30.0 17.4 %collective-permute-done = s32[8,4,1024]{2,1,0:T(4,128)S(1)} collective-permute-done((s32[8,4,1024]{2,1,0:T(4,128)}, s32[8,4,1024]{2,1,0:T(4,128)S(1)}, u32[]{:S(2)}, u32[]{:S(2)}) %collective-permute-start) | collective-permute-done | bytes 131104 | tf_op jit(solution)/shard_map/ppermute | solution.py:636
  47.4 1.3 collective-permute-start.3
  48.8 2.3 %collective-permute-done.2 = s32[64,1024]{1,0:T(8,128)S(1)} collective-permute-done((s32[64,1024]{1,0:T(8,128)}, s32[64,1024]{1,0:T(8,128)S(1)}, u32[]{:S(2)}, u32[]{:S(2)}) %collective-permute-start.2) | collective-permute-done | bytes 262176 | tf_op jit(solution)/shard_map/ppermute | solution.py:636
  51.1 1.4 collective-permute-done.3
  52.5 1.6 copy-done
  54.1 1.8 %shard_map.87.code = s32[8,72,1024]{2,1,0:T(8,128)S(1)} custom-call(s32[8,64,1024]{2,1,0:T(8,128)S(1)} %copy-done, s32[8,8,1024]{2,1,0:T(8,128)S(1)} %pad_add_fusion.tile, s32[72,1024]{1,0:T(8,128)S(1)} %constant_dynamic-update-slice_fusion.beyond), custom_call_target="tpu_custom_call" | custom-call | flops 300000000 | bytes 1048576 | tf_op jit(solution)/shard_map/pallas_call | solution.py:356
  57.1 5.7 %shard_map.88 = (f32[16904,128]{1,0:T(8,128)S(1)}, f32[768,128]{1,0:T(8,128)S(1)}, f32[768,128]{1,0:T(8,128)S(1)}) custom-call(f32[4224,128]{1,0:T(8,128)} %bitcast.5.arr_hbm, s32[1024]{0:T(1024)S(1)} %convert_element_type.8.names), custom_call_target="tpu_custom_call" | custom-call | flops 300000000 | bytes 1048576 | tf_op jit(solution)/shard_map/pallas_call | solution.py:246
  62.8 1.9 %collective-permute-start.4 = (f32[768,128]{1,0:T(8,128)S(1)}, f32[768,128]{1,0:T(8,128)S(1)}, u32[]{:S(2)}, u32[]{:S(2)}) collective-permute-start(f32[768,128]{1,0:T(8,128)S(1)} %get-tuple-element.49), channel_id=1, source_target_pairs={{1,0},{2,1},{3,2},{4,3},{5,4},{6,5},{7,6},{9,8},{10,9},{11,10},{12... | collective-permute-start | bytes 1179656 | tf_op jit(solution)/shard_map/ppermute | solution.py:636
  64.7 3.6 %collective-permute-start.5 = (f32[768,128]{1,0:T(8,128)S(1)}, f32[768,128]{1,0:T(8,128)S(1)}, u32[]{:S(2)}, u32[]{:S(2)}) collective-permute-start(f32[768,128]{1,0:T(8,128)S(1)} %get-tuple-element.50), channel_id=1, source_target_pairs={{0,1},{1,2},{2,3},{3,4},{4,5},{5,6},{6,7},{8,9},{9,10},{10,11},{11... | collective-permute-start | bytes 1179656 | tf_op jit(solution)/shard_map/ppermute | solution.py:636
  68.4 1.9 %shard_map.89 = (f32[3,8,72,1024]{3,2,1,0:T(8,128)S(1)}, f32[8,72,1024]{2,1,0:T(8,128)S(1)}, f32[3,8,72,1024]{3,2,1,0:T(8,128)S(1)}) custom-call(f32[16904,128]{1,0:T(8,128)S(1)} %get-tuple-element.52.tot, s32[8,72,1024]{2,1,0:T(8,128)S(1)} %shard_map.87.code), custom_call_target="tpu_custom_call" | custom-call | flops 300000000 | bytes 1048576 | tf_op jit(solution)/shard_map/pallas_call | solution.py:402
  70.3 1.6 collective-permute-done.4.after
  74.0 2.8 %collective-permute-start.6 = (f32[72,1024]{1,0:T(8,128)S(1)}, f32[72,1024]{1,0:T(8,128)S(1)}, u32[]{:S(2)}, u32[]{:S(2)}) collective-permute-start(f32[72,1024]{1,0:T(8,128)S(1)} %get-tuple-element.56), channel_id=1, source_target_pairs={{0,8},{8,16},{16,24},{24,32},{32,40},{40,48},{48,56},{56,64},{64,7... | collective-permute-start | bytes 884744 | tf_op jit(solution)/shard_map/ppermute | solution.py:636
  76.9 1.3 collective-permute-start.7
  78.2 3.3 %shard_map.91 = (f32[8,72,1024]{2,1,0:T(8,128)S(1)}, f32[3,8,72,1024]{3,2,1,0:T(8,128)S(1)}) custom-call(f32[3,8,72,1024]{3,2,1,0:T(8,128)S(1)} %get-tuple-element.59.v_in, s32[8,72,1024]{2,1,0:T(8,128)S(1)} %shard_map.87.code, f32[3,8,72,1024]{3,2,1,0:T(8,128)S(1)} %get-tuple-element.60.guess, ...), custom_call_target="tpu_custom_call", output_to_operand_aliasing={{1}: (0, {})} | custom-call | flops 300000000 | bytes 1048576 | tf_op jit(solution)/shard_map/pallas_call | solution.py:583
  81.5 2.9 %collective-permute-done.7.spread = f32[72,1024]{1,0:T(8,128)S(1)} collective-permute-done((f32[72,1024]{1,0:T(8,128)S(1)}, f32[72,1024]{1,0:T(8,128)S(1)}, u32[]{:S(2)}, u32[]{:S(2)}) %collective-permute-start.7) | collective-permute-done | bytes 294944 | tf_op jit(solution)/shard_map/ppermute | solution.py:636
  85.1 4.6 %collective-permute-start.8 = (f32[72,1024]{1,0:T(8,128)S(1)}, f32[72,1024]{1,0:T(8,128)S(1)}, u32[]{:S(2)}, u32[]{:S(2)}) collective-permute-start(f32[72,1024]{1,0:T(8,128)S(1)} %get-tuple-element.64), channel_id=1, source_target_pairs={{0,8},{8,16},{16,24},{24,32},{32,40},{40,48},{48,56},{56,64},{64,7... | collective-permute-start | bytes 884744 | tf_op jit(solution)/shard_map/ppermute | solution.py:636
  89.7 1.3 collective-permute-start.9
  91.0 3.5 %shard_map.93 = (f32[8,72,1024]{2,1,0:T(8,128)S(1)}, f32[3,8,72,1024]{3,2,1,0:T(8,128)S(1)}) custom-call(f32[8,72,1024]{2,1,0:T(8,128)S(1)} %get-tuple-element.67.p_in, f32[3,8,72,1024]{3,2,1,0:T(8,128)S(1)} %get-tuple-element.68.v_in, s32[8,72,1024]{2,1,0:T(8,128)S(1)} %shard_map.87.code, ...), custom_call_target="tpu_custom_call", output_to_operand_aliasing={{0}: (0, {}), {1}: (1, {})} | custom-call | flops 300000000 | bytes 1048576 | tf_op jit(solution)/shard_map/pallas_call | solution.py:595
  94.6 3.7 %collective-permute-done.9.spread = f32[72,1024]{1,0:T(8,128)S(1)} collective-permute-done((f32[72,1024]{1,0:T(8,128)S(1)}, f32[72,1024]{1,0:T(8,128)S(1)}, u32[]{:S(2)}, u32[]{:S(2)}) %collective-permute-start.9) | collective-permute-done | bytes 294944 | tf_op jit(solution)/shard_map/ppermute | solution.py:636
  99.2 3.8 %collective-permute-start.10 = (f32[72,1024]{1,0:T(8,128)S(1)}, f32[72,1024]{1,0:T(8,128)S(1)}, u32[]{:S(2)}, u32[]{:S(2)}) collective-permute-start(f32[72,1024]{1,0:T(8,128)S(1)} %get-tuple-element.71), channel_id=1, source_target_pairs={{0,8},{8,16},{16,24},{24,32},{32,40},{40,48},{48,56},{56,64},{64,7... | collective-permute-start | bytes 884744 | tf_op jit(solution)/shard_map/ppermute | solution.py:636
  102.9 1.3 collective-permute-start.11
  104.2 6.4 %shard_map.95 = (f32[8,72,1024]{2,1,0:T(8,128)S(1)}, f32[3,8,72,1024]{3,2,1,0:T(8,128)S(1)}, f32[16904,128]{1,0:T(8,128)S(1)}, f32[8,64,1024]{2,1,0:T(8,128)}, f32[3,8,64,1024]{3,2,1,0:T(8,128)}) custom-call(f32[8,72,1024]{2,1,0:T(8,128)S(1)} %get-tuple-element.74.p_in, ...), custom_call_target="tpu_custom_call", output_to_operand_aliasing={{0}: (0, {}), {1}: (1, {})} | custom-call | flops 500000000 | bytes 1048576 | tf_op jit(solution)/shard_map/pallas_call | solution.py:610
  110.6 2.3 %collective-permute-done.11.spread = f32[72,1024]{1,0:T(8,128)S(1)} collective-permute-done((f32[72,1024]{1,0:T(8,128)S(1)}, f32[72,1024]{1,0:T(8,128)S(1)}, u32[]{:S(2)}, u32[]{:S(2)}) %collective-permute-start.11) | collective-permute-done | bytes 294944 | tf_op jit(solution)/shard_map/ppermute | solution.py:636
  112.9 3.6 %shard_map.96 = (f32[8,72,1024]{2,1,0:T(8,128)S(1)}, f32[3,8,72,1024]{3,2,1,0:T(8,128)S(1)}, f32[16904,128]{1,0:T(8,128)S(1)}, f32[8,64,1024]{2,1,0:T(8,128)}, f...) custom-call(f32[72,1024]{1,0:T(8,128)S(1)} %collective-permute-done., ...), custom_call_target="tpu_custom_call", output_to_operand_aliasing={{2}: (5, {}), {0}: (6, {}), {1}: (7, {}), {3}: (11, {}), {4... | custom-call | flops 300000000 | bytes 1048576 | tf_op jit(solution)/shard_map/pallas_call | solution.py:620
  116.6 39.2 %all_to_all.10 = f32[128,24,128]{2,1,0:T(8,128)S(1)} all-to-all(f32[128,24,128]{2,1,0:T(8,128)S(1)} %bitcast.11), channel_id=1, replica_groups=mesh['slab'=16,'sub'=8] {'slab','sub'}, dimensions={0} | all-to-all | bytes 3145728 | tf_op jit(solution)/shard_map/all_to_all | solution.py:664
  155.8 5.1 %shard_map.97 = f32[3,512,128]{2,1,0:T(8,128)} custom-call(f32[3072,128]{1,0:T(8,128)S(1)} %bitcast.10, f32[3,512,128]{2,1,0:T(8,128)S(1)} %bitcast.13, s32[512,128]{1,0:T(8,128)S(1)} %copy-done.2, s32[512]{0:T(512)S(1)} %copy-done.3), custom_call_target="tpu_custom_call" | custom-call | flops 600000000 | bytes 1048576 | tf_op jit(solution)/shard_map/pallas_call | solution.py:195
  (22 shorter events, 5.0 us)
Async XLA Ops:
  9.3 46.6 %all-to-all-start = ((f32[128,1,4224]{2,1,0:T(1,128)}), f32[128,1,4224]{2,1,0:T(1,128)}, u32[]{:S(2)}, u32[]{:S(2)}) async-start(f32[128,1,4224]{2,1,0:T(1,128)} %bitcast.14), calls=%async_computation | async-start | bytes 4325376 | tf_op jit(solution)/shard_map/all_to_all | solution.py:654
  23.2 24.3 %collective-permute-start = (s32[8,4,1024]{2,1,0:T(4,128)}, s32[8,4,1024]{2,1,0:T(4,128)S(1)}, u32[]{:S(2)}, u32[]{:S(2)}) collective-permute-start(s32[8,4,1024]{2,1,0:T(4,128)} %get-tuple-element.45), channel_id=1, source_target_pairs={{1,0},{2,1},{3,2},{4,3},{5,4},{6,5},{7,6},{9,8},{10,9},{11,10},{12... | collective-permute-start | bytes 393224 | tf_op jit(solution)/shard_map/ppermute | solution.py:636
  26.2 21.2 %collective-permute-start.1 = (s32[8,4,1024]{2,1,0:T(4,128)}, s32[8,4,1024]{2,1,0:T(4,128)S(1)}, u32[]{:S(2)}, u32[]{:S(2)}) collective-permute-start(s32[8,4,1024]{2,1,0:T(4,128)} %get-tuple-element.46), channel_id=1, source_target_pairs={{0,1},{1,2},{2,3},{3,4},{4,5},{5,6},{6,7},{8,9},{9,10},{10,11},{11... | collective-permute-start | bytes 393224 | tf_op jit(solution)/shard_map/ppermute | solution.py:636
  28.7 22.3 %collective-permute-start.2 = (s32[64,1024]{1,0:T(8,128)}, s32[64,1024]{1,0:T(8,128)S(1)}, u32[]{:S(2)}, u32[]{:S(2)}) collective-permute-start(s32[64,1024]{1,0:T(8,128)} %get-tuple-element.47), channel_id=1, source_target_pairs={{8,0},{16,8},{24,16},{32,24},{40,32},{48,40},{56,48},{64,56},{72,6... | collective-permute-start | bytes 786440 | tf_op jit(solution)/shard_map/ppermute | solution.py:636
  47.4 5.1 %collective-permute-start.3 = (s32[8,1024]{1,0:T(8,128)S(1)}, s32[8,1024]{1,0:T(8,128)S(1)}, u32[]{:S(2)}, u32[]{:S(2)}) collective-permute-start(s32[8,1024]{1,0:T(8,128)S(1)} %fusion.1), channel_id=1, source_target_pairs={{8,0},{16,8},{24,16},{32,24},{40,32},{48,40},{56,48},{64,56},{72,6... | collective-permute-start | bytes 98312 | tf_op jit(solution)/shard_map/ppermute | solution.py:636
  52.5 1.6 copy-start
  62.8 9.1 %collective-permute-start.4 = (f32[768,128]{1,0:T(8,128)S(1)}, f32[768,128]{1,0:T(8,128)S(1)}, u32[]{:S(2)}, u32[]{:S(2)}) collective-permute-start(f32[768,128]{1,0:T(8,128)S(1)} %get-tuple-element.49), channel_id=1, source_target_pairs={{1,0},{2,1},{3,2},{4,3},{5,4},{6,5},{7,6},{9,8},{10,9},{11,10},{12... | collective-permute-start | bytes 1179656 | tf_op jit(solution)/shard_map/ppermute | solution.py:636
  64.7 8.3 %collective-permute-start.5 = (f32[768,128]{1,0:T(8,128)S(1)}, f32[768,128]{1,0:T(8,128)S(1)}, u32[]{:S(2)}, u32[]{:S(2)}) collective-permute-start(f32[768,128]{1,0:T(8,128)S(1)} %get-tuple-element.50), channel_id=1, source_target_pairs={{0,1},{1,2},{2,3},{3,4},{4,5},{5,6},{6,7},{8,9},{9,10},{10,11},{11... | collective-permute-start | bytes 1179656 | tf_op jit(solution)/shard_map/ppermute | solution.py:636
  74.0 7.5 %collective-permute-start.6 = (f32[72,1024]{1,0:T(8,128)S(1)}, f32[72,1024]{1,0:T(8,128)S(1)}, u32[]{:S(2)}, u32[]{:S(2)}) collective-permute-start(f32[72,1024]{1,0:T(8,128)S(1)} %get-tuple-element.56), channel_id=1, source_target_pairs={{0,8},{8,16},{16,24},{24,32},{32,40},{40,48},{48,56},{56,64},{64,7... | collective-permute-start | bytes 884744 | tf_op jit(solution)/shard_map/ppermute | solution.py:636
  76.9 7.5 %collective-permute-start.7 = (f32[72,1024]{1,0:T(8,128)S(1)}, f32[72,1024]{1,0:T(8,128)S(1)}, u32[]{:S(2)}, u32[]{:S(2)}) collective-permute-start(f32[72,1024]{1,0:T(8,128)S(1)} %get-tuple-element.57), channel_id=1, source_target_pairs={{8,0},{16,8},{24,16},{32,24},{40,32},{48,40},{56,48},{64,56},{72,6... | collective-permute-start | bytes 884744 | tf_op jit(solution)/shard_map/ppermute | solution.py:636
  85.1 9.4 %collective-permute-start.8 = (f32[72,1024]{1,0:T(8,128)S(1)}, f32[72,1024]{1,0:T(8,128)S(1)}, u32[]{:S(2)}, u32[]{:S(2)}) collective-permute-start(f32[72,1024]{1,0:T(8,128)S(1)} %get-tuple-element.64), channel_id=1, source_target_pairs={{0,8},{8,16},{16,24},{24,32},{32,40},{40,48},{48,56},{56,64},{64,7... | collective-permute-start | bytes 884744 | tf_op jit(solution)/shard_map/ppermute | solution.py:636
  89.7 8.6 %collective-permute-start.9 = (f32[72,1024]{1,0:T(8,128)S(1)}, f32[72,1024]{1,0:T(8,128)S(1)}, u32[]{:S(2)}, u32[]{:S(2)}) collective-permute-start(f32[72,1024]{1,0:T(8,128)S(1)} %get-tuple-element.65), channel_id=1, source_target_pairs={{8,0},{16,8},{24,16},{32,24},{40,32},{48,40},{56,48},{64,56},{72,6... | collective-permute-start | bytes 884744 | tf_op jit(solution)/shard_map/ppermute | solution.py:636
  99.2 11.4 %collective-permute-start.10 = (f32[72,1024]{1,0:T(8,128)S(1)}, f32[72,1024]{1,0:T(8,128)S(1)}, u32[]{:S(2)}, u32[]{:S(2)}) collective-permute-start(f32[72,1024]{1,0:T(8,128)S(1)} %get-tuple-element.71), channel_id=1, source_target_pairs={{0,8},{8,16},{16,24},{24,32},{32,40},{40,48},{48,56},{56,64},{64,7... | collective-permute-start | bytes 884744 | tf_op jit(solution)/shard_map/ppermute | solution.py:636
  102.9 10.0 %collective-permute-start.11 = (f32[72,1024]{1,0:T(8,128)S(1)}, f32[72,1024]{1,0:T(8,128)S(1)}, u32[]{:S(2)}, u32[]{:S(2)}) collective-permute-start(f32[72,1024]{1,0:T(8,128)S(1)} %get-tuple-element.72), channel_id=1, source_target_pairs={{8,0},{16,8},{24,16},{32,24},{40,32},{48,40},{56,48},{64,56},{72,6... | collective-permute-start | bytes 884744 | tf_op jit(solution)/shard_map/ppermute | solution.py:636
  116.5 39.2 %copy-start.1 = (f32[512,3,128]{2,0,1:T(8,128)S(1)}, f32[512,3,128]{2,0,1:T(8,128)}, u32[]{:S(2)}) copy-start(f32[512,3,128]{2,0,1:T(8,128)} %param.6) | copy-start | bytes 2359300
  116.5 39.2 %copy-start.2 = (s32[512,128]{1,0:T(8,128)S(1)}, s32[512,128]{1,0:T(8,128)}, u32[]{:S(2)}) copy-start(s32[512,128]{1,0:T(8,128)} %offset.1) | copy-start | bytes 786436
  116.6 39.2 %copy-start.3 = (s32[512]{0:T(512)S(1)}, s32[512]{0:T(512)}, u32[]{:S(2)}) copy-start(s32[512]{0:T(512)} %get-tuple-element.82.place) | copy-start | bytes 6148

commit v3 on v2

--- a/solution.py
+++ b/solution.py
@@ -650,14 +650,16 @@
     planes = velocity.transpose(1, 0, 2)
     outgoing, place = splat(planes, weight, offset, owner[:, 0], brick[:, 0], devices)
     tile = jnp.concatenate([later, prior], 1)
-    beyond = jnp.concatenate([beyond_own, shifted(tile[0], "slab", -1)], 0)
+    beyond_edge = shifted(tile[0], "slab", -1)
     arrived = lax.all_to_all(outgoing.reshape(devices, 1, CHUNK * LANES), both, 0, 0, tiled=True)
-    code = make_code(flags, tile, beyond)
-    arrived, code, beyond = lax.optimization_barrier((arrived, code, beyond))
+    arrived, tile = lax.optimization_barrier((arrived, tile))
     names = arrived[:, 0, 32 * LANES : 32 * LANES + 8].astype(I32).reshape(-1)
     totals, first_rows, last_rows = scatter(arrived.reshape(devices * CHUNK, LANES), names, xs, ys)
     after = shifted(first_rows, "sub", -1)
     before = shifted(last_rows, "sub", 1)
+    totals, tile, beyond_own, beyond_edge = lax.optimization_barrier((totals, tile, beyond_own, beyond_edge))
+    beyond = jnp.concatenate([beyond_own, beyond_edge], 0)
+    code = make_code(flags, tile, beyond)
     guess, inverse, v = fields(totals, code)
     guess, inverse, v, to_next, to_prior = add_edge(after, before, code, guess, inverse, v)
     p, v, reply = climb(names, v, code, guess, inverse, beyond, to_next, to_prior)

time: 162 us -> 163 us (level)
    all_to_all x1, waiting for transfers between devices: 0.01 us -> 4.59 us  [on_device(): lax.all_to_all(outgoing.reshape(devices, 1, CHUNK * LANES), both, 0, 0, t...]
    ppermute x12, waiting for transfers between devices: 32.7 us -> 29.3 us  [shifted(): lax.ppermute(block, axis, [(i - distance, i) for i in devices if i - dist...]
  transfers between devices with their start and end apart: 13 -> 13, of which waited for: 8 -> 8; matrix products, arithmetic and copies ran while one was open for 0% -> 1% of each run, Pallas kernels for 12% -> 15%
where the time goes in v3:
time: 163 us; the launch traced here: 162 us
  Pallas kernels  44.4 us (27%)
  starting transfers between devices  41.1 us (25%)
  blocking collectives  40.6 us (25%)
  waiting for transfers between devices  33.9 us (21%)
    all_to_all x1, blocking collectives, on_device(): lax.all_to_all(reply.reshape(devices, 24, LANES), both, 0, 0, tiled=True)  40.6 us
    ppermute x12, waiting for transfers between devices, shifted(): lax.ppermute(block, axis, [(i - distance, i) for i in devices if i - dist...  29.3 us
    ppermute x12, starting transfers between devices, shifted(): lax.ppermute(block, axis, [(i - distance, i) for i in devices if i - dist...  29.2 us
    all_to_all x1, starting transfers between devices, on_device(): lax.all_to_all(outgoing.reshape(devices, 1, CHUNK * LANES), both, 0, 0, t...  11.9 us
    pallas_call x1, Pallas kernels, splat(): call(splat_kernel, [hbm()] * 5, [vmem(), smem()], [jax.ShapeDtypeStruct((...  8.66 us
    pallas_call x1, Pallas kernels, climb(): call(inner_last_kernel, [vmem()] * 5, [vmem()] * 3 + [hbm()] * 2, like(p,...  6.37 us
    pallas_call x1, Pallas kernels, scatter(): call(scatter_kernel, [hbm(), smem()], [vmem()] * 3, [jax.ShapeDtypeStruct...  5.73 us
    pallas_call x1, Pallas kernels, pick(): call(pick_kernel, [vmem()] * 3 + [smem()], vmem(), jax.ShapeDtypeStruct((...  5.07 us
  transfers between devices with their start and end apart: 13, of which 8 were waited for; matrix products, arithmetic and copies ran while one was open for 1% of the time, Pallas kernels for 15%

profile of v3, /device:TPU:1, one launch (start us, length us, event | category | flops | bytes accessed | tf_op | source)
XLA Modules:
  0.0 162.2 jit_solution(11993485722457262683)
XLA Ops:
  0.6 8.7 %shard_map.85 = (f32[4224,128]{1,0:T(8,128)}, s32[512]{0:T(512)}) custom-call(f32[3,512,128]{2,1,0:T(8,128)} %bitcast.12, f32[512,128]{1,0:T(8,128)} %weight_hbm.1, s32[512,128]{1,0:T(8,128)} %offset.1, s32[512]{0:T(512)} %bitcast.16, s32[512]{0:T(512)} %bitcast.17), custom_call_target="tpu_custom_call" | custom-call | flops 800000000 | bytes 1048576 | tf_op jit(solution)/shard_map/pallas_call | solution.py:127
  9.3 11.9 %all-to-all-start = ((f32[128,1,4224]{2,1,0:T(1,128)}), f32[128,1,4224]{2,1,0:T(1,128)}, u32[]{:S(2)}, u32[]{:S(2)}) async-start(f32[128,1,4224]{2,1,0:T(1,128)} %bitcast.14), calls=%async_computation | async-start | bytes 4325376 | tf_op jit(solution)/shard_map/all_to_all | solution.py:654
  21.2 2.0 %shard_map.86 = (s32[64,1024]{1,0:T(8,128)}, s32[8,4,1024]{2,1,0:T(4,128)}, s32[8,4,1024]{2,1,0:T(4,128)}) custom-call(s32[8,64,1024]{2,1,0:T(8,128)} %flags.3), custom_call_target="tpu_custom_call" | custom-call | flops 100000000 | bytes 1048576 | tf_op jit(solution)/shard_map/pallas_call | solution.py:316
  23.2 3.2 %collective-permute-start = (s32[8,4,1024]{2,1,0:T(4,128)}, s32[8,4,1024]{2,1,0:T(4,128)S(1)}, u32[]{:S(2)}, u32[]{:S(2)}) collective-permute-start(s32[8,4,1024]{2,1,0:T(4,128)} %get-tuple-element.48), channel_id=1, source_target_pairs={{1,0},{2,1},{3,2},{4,3},{5,4},{6,5},{7,6},{9,8},{10,9},{11,10},{12... | collective-permute-start | bytes 393224 | tf_op jit(solution)/shard_map/ppermute | solution.py:636
  26.4 2.5 %collective-permute-start.1 = (s32[8,4,1024]{2,1,0:T(4,128)}, s32[8,4,1024]{2,1,0:T(4,128)S(1)}, u32[]{:S(2)}, u32[]{:S(2)}) collective-permute-start(s32[8,4,1024]{2,1,0:T(4,128)} %get-tuple-element.49), channel_id=1, source_target_pairs={{0,1},{1,2},{2,3},{3,4},{4,5},{5,6},{6,7},{8,9},{9,10},{10,11},{11... | collective-permute-start | bytes 393224 | tf_op jit(solution)/shard_map/ppermute | solution.py:636
  28.9 1.3 collective-permute-start.4
  30.2 17.2 %collective-permute-done = s32[8,4,1024]{2,1,0:T(4,128)S(1)} collective-permute-done((s32[8,4,1024]{2,1,0:T(4,128)}, s32[8,4,1024]{2,1,0:T(4,128)S(1)}, u32[]{:S(2)}, u32[]{:S(2)}) %collective-permute-start) | collective-permute-done | bytes 131104 | tf_op jit(solution)/shard_map/ppermute | solution.py:636
  47.5 4.6 %all-to-all-done = f32[128,1,4224]{2,1,0:T(1,128)} async-done(((f32[128,1,4224]{2,1,0:T(1,128)}), f32[128,1,4224]{2,1,0:T(1,128)}, u32[]{:S(2)}, u32[]{:S(2)}) %all-to-all-start) | async-done | bytes 2162720 | tf_op jit(solution)/shard_map/all_to_all | solution.py:654
  52.1 1.0 convert_reduce_fusion
  53.2 5.7 %shard_map.87 = (f32[16904,128]{1,0:T(8,128)S(1)}, f32[768,128]{1,0:T(8,128)S(1)}, f32[768,128]{1,0:T(8,128)S(1)}) custom-call(f32[4224,128]{1,0:T(8,128)} %bitcast.4.arr_hbm, s32[1024]{0:T(1024)S(1)} %convert_element_type.8.names), custom_call_target="tpu_custom_call" | custom-call | flops 300000000 | bytes 1048576 | tf_op jit(solution)/shard_map/pallas_call | solution.py:246
  58.9 3.5 %collective-permute-start.2 = (f32[768,128]{1,0:T(8,128)S(1)}, f32[768,128]{1,0:T(8,128)S(1)}, u32[]{:S(2)}, u32[]{:S(2)}) collective-permute-start(f32[768,128]{1,0:T(8,128)S(1)} %get-tuple-element.51), channel_id=1, source_target_pairs={{1,0},{2,1},{3,2},{4,3},{5,4},{6,5},{7,6},{9,8},{10,9},{11,10},{12... | collective-permute-start | bytes 1179656 | tf_op jit(solution)/shard_map/ppermute | solution.py:636
  62.4 2.1 %collective-permute-start.3 = (f32[768,128]{1,0:T(8,128)S(1)}, f32[768,128]{1,0:T(8,128)S(1)}, u32[]{:S(2)}, u32[]{:S(2)}) collective-permute-start(f32[768,128]{1,0:T(8,128)S(1)} %get-tuple-element.52), channel_id=1, source_target_pairs={{0,1},{1,2},{2,3},{3,4},{4,5},{5,6},{6,7},{8,9},{9,10},{10,11},{11... | collective-permute-start | bytes 1179656 | tf_op jit(solution)/shard_map/ppermute | solution.py:636
  64.5 1.3 collective-permute-start.5
  65.8 3.4 %collective-permute-done.5 = s32[8,1024]{1,0:T(8,128)S(1)} collective-permute-done((s32[8,1024]{1,0:T(8,128)S(1)}, s32[8,1024]{1,0:T(8,128)S(1)}, u32[]{:S(2)}, u32[]{:S(2)}) %collective-permute-start.5) | collective-permute-done | bytes 32800 | tf_op jit(solution)/shard_map/ppermute | solution.py:636
  69.2 1.8 %shard_map.88.code = s32[8,72,1024]{2,1,0:T(8,128)S(1)} custom-call(s32[8,64,1024]{2,1,0:T(8,128)S(1)} %copy-done, s32[8,8,1024]{2,1,0:T(8,128)S(1)} %pad_add_fusion.tile, s32[72,1024]{1,0:T(8,128)S(1)} %constant_dynamic-update-slice_fusion.beyond), custom_call_target="tpu_custom_call" | custom-call | flops 300000000 | bytes 1048576 | tf_op jit(solution)/shard_map/pallas_call | solution.py:356
  71.1 1.9 %shard_map.89 = (f32[3,8,72,1024]{3,2,1,0:T(8,128)S(1)}, f32[8,72,1024]{2,1,0:T(8,128)S(1)}, f32[3,8,72,1024]{3,2,1,0:T(8,128)S(1)}) custom-call(f32[16904,128]{1,0:T(8,128)S(1)} %get-tuple-element.59.tot, s32[8,72,1024]{2,1,0:T(8,128)S(1)} %shard_map.88.code), custom_call_target="tpu_custom_call" | custom-call | flops 300000000 | bytes 1048576 | tf_op jit(solution)/shard_map/pallas_call | solution.py:402
  73.0 0.9 shard_map.90
  73.9 1.6 %collective-permute-start.6 = (f32[72,1024]{1,0:T(8,128)S(1)}, f32[72,1024]{1,0:T(8,128)S(1)}, u32[]{:S(2)}, u32[]{:S(2)}) collective-permute-start(f32[72,1024]{1,0:T(8,128)S(1)} %get-tuple-element.63), channel_id=1, source_target_pairs={{0,8},{8,16},{16,24},{24,32},{32,40},{40,48},{48,56},{56,64},{64,7... | collective-permute-start | bytes 884744 | tf_op jit(solution)/shard_map/ppermute | solution.py:636
  75.6 1.3 collective-permute-start.7
  76.9 3.3 %shard_map.91 = (f32[8,72,1024]{2,1,0:T(8,128)S(1)}, f32[3,8,72,1024]{3,2,1,0:T(8,128)S(1)}) custom-call(f32[3,8,72,1024]{3,2,1,0:T(8,128)S(1)} %get-tuple-element.65.v_in, s32[8,72,1024]{2,1,0:T(8,128)S(1)} %shard_map.88.code, f32[3,8,72,1024]{3,2,1,0:T(8,128)S(1)} %get-tuple-element.66.guess, ...), custom_call_target="tpu_custom_call", output_to_operand_aliasing={{1}: (0, {})} | custom-call | flops 300000000 | bytes 1048576 | tf_op jit(solution)/shard_map/pallas_call | solution.py:583
  80.7 3.9 %collective-permute-done.7.spread = f32[72,1024]{1,0:T(8,128)S(1)} collective-permute-done((f32[72,1024]{1,0:T(8,128)S(1)}, f32[72,1024]{1,0:T(8,128)S(1)}, u32[]{:S(2)}, u32[]{:S(2)}) %collective-permute-start.7) | collective-permute-done | bytes 294944 | tf_op jit(solution)/shard_map/ppermute | solution.py:636
  85.3 5.9 %collective-permute-start.8 = (f32[72,1024]{1,0:T(8,128)S(1)}, f32[72,1024]{1,0:T(8,128)S(1)}, u32[]{:S(2)}, u32[]{:S(2)}) collective-permute-start(f32[72,1024]{1,0:T(8,128)S(1)} %get-tuple-element.70), channel_id=1, source_target_pairs={{0,8},{8,16},{16,24},{24,32},{32,40},{40,48},{48,56},{56,64},{64,7... | collective-permute-start | bytes 884744 | tf_op jit(solution)/shard_map/ppermute | solution.py:636
  91.1 1.3 collective-permute-start.9
  92.4 3.5 %shard_map.93 = (f32[8,72,1024]{2,1,0:T(8,128)S(1)}, f32[3,8,72,1024]{3,2,1,0:T(8,128)S(1)}) custom-call(f32[8,72,1024]{2,1,0:T(8,128)S(1)} %get-tuple-element.73.p_in, f32[3,8,72,1024]{3,2,1,0:T(8,128)S(1)} %get-tuple-element.74.v_in, s32[8,72,1024]{2,1,0:T(8,128)S(1)} %shard_map.88.code, ...), custom_call_target="tpu_custom_call", output_to_operand_aliasing={{0}: (0, {}), {1}: (1, {})} | custom-call | flops 300000000 | bytes 1048576 | tf_op jit(solution)/shard_map/pallas_call | solution.py:595
  96.2 3.9 %collective-permute-done.9.spread = f32[72,1024]{1,0:T(8,128)S(1)} collective-permute-done((f32[72,1024]{1,0:T(8,128)S(1)}, f32[72,1024]{1,0:T(8,128)S(1)}, u32[]{:S(2)}, u32[]{:S(2)}) %collective-permute-start.9) | collective-permute-done | bytes 294944 | tf_op jit(solution)/shard_map/ppermute | solution.py:636
  100.1 0.8 shard_map.94
  100.9 4.0 %collective-permute-start.10 = (f32[72,1024]{1,0:T(8,128)S(1)}, f32[72,1024]{1,0:T(8,128)S(1)}, u32[]{:S(2)}, u32[]{:S(2)}) collective-permute-start(f32[72,1024]{1,0:T(8,128)S(1)} %get-tuple-element.77), channel_id=1, source_target_pairs={{0,8},{8,16},{16,24},{24,32},{32,40},{40,48},{48,56},{56,64},{64,7... | collective-permute-start | bytes 884744 | tf_op jit(solution)/shard_map/ppermute | solution.py:636
  104.9 1.3 collective-permute-start.11
  106.2 6.4 %shard_map.95 = (f32[8,72,1024]{2,1,0:T(8,128)S(1)}, f32[3,8,72,1024]{3,2,1,0:T(8,128)S(1)}, f32[16904,128]{1,0:T(8,128)S(1)}, f32[8,64,1024]{2,1,0:T(8,128)}, f32[3,8,64,1024]{3,2,1,0:T(8,128)}) custom-call(f32[8,72,1024]{2,1,0:T(8,128)S(1)} %get-tuple-element.80.p_in, ...), custom_call_target="tpu_custom_call", output_to_operand_aliasing={{0}: (0, {}), {1}: (1, {})} | custom-call | flops 500000000 | bytes 1048576 | tf_op jit(solution)/shard_map/pallas_call | solution.py:610
  112.9 3.6 %shard_map.96 = (f32[8,72,1024]{2,1,0:T(8,128)S(1)}, f32[3,8,72,1024]{3,2,1,0:T(8,128)S(1)}, f32[16904,128]{1,0:T(8,128)S(1)}, f32[8,64,1024]{2,1,0:T(8,128)}, f...) custom-call(f32[72,1024]{1,0:T(8,128)S(1)} %collective-permute-done., ...), custom_call_target="tpu_custom_call", output_to_operand_aliasing={{2}: (5, {}), {0}: (6, {}), {1}: (7, {}), {3}: (11, {}), {4... | custom-call | flops 300000000 | bytes 1048576 | tf_op jit(solution)/shard_map/pallas_call | solution.py:620
  116.5 40.6 %all_to_all.10 = f32[128,24,128]{2,1,0:T(8,128)S(1)} all-to-all(f32[128,24,128]{2,1,0:T(8,128)S(1)} %bitcast.11), channel_id=1, replica_groups=mesh['slab'=16,'sub'=8] {'slab','sub'}, dimensions={0} | all-to-all | bytes 3145728 | tf_op jit(solution)/shard_map/all_to_all | solution.py:666
  157.2 5.1 %shard_map.97 = f32[3,512,128]{2,1,0:T(8,128)} custom-call(f32[3072,128]{1,0:T(8,128)S(1)} %bitcast.10, f32[3,512,128]{2,1,0:T(8,128)S(1)} %bitcast.13, s32[512,128]{1,0:T(8,128)S(1)} %copy-done.2, s32[512]{0:T(512)S(1)} %copy-done.3), custom_call_target="tpu_custom_call" | custom-call | flops 600000000 | bytes 1048576 | tf_op jit(solution)/shard_map/pallas_call | solution.py:195
  (22 shorter events, 1.9 us)
Async XLA Ops:
  9.3 42.8 %all-to-all-start = ((f32[128,1,4224]{2,1,0:T(1,128)}), f32[128,1,4224]{2,1,0:T(1,128)}, u32[]{:S(2)}, u32[]{:S(2)}) async-start(f32[128,1,4224]{2,1,0:T(1,128)} %bitcast.14), calls=%async_computation | async-start | bytes 4325376 | tf_op jit(solution)/shard_map/all_to_all | solution.py:654
  23.2 46.1 %copy-start = (s32[8,64,1024]{2,1,0:T(8,128)S(1)}, s32[8,64,1024]{2,1,0:T(8,128)}, u32[]{:S(2)}) copy-start(s32[8,64,1024]{2,1,0:T(8,128)} %flags.3) | copy-start | bytes 6291460
  23.2 24.2 %collective-permute-start = (s32[8,4,1024]{2,1,0:T(4,128)}, s32[8,4,1024]{2,1,0:T(4,128)S(1)}, u32[]{:S(2)}, u32[]{:S(2)}) collective-permute-start(s32[8,4,1024]{2,1,0:T(4,128)} %get-tuple-element.48), channel_id=1, source_target_pairs={{1,0},{2,1},{3,2},{4,3},{5,4},{6,5},{7,6},{9,8},{10,9},{11,10},{12... | collective-permute-start | bytes 393224 | tf_op jit(solution)/shard_map/ppermute | solution.py:636
  26.4 21.1 %collective-permute-start.1 = (s32[8,4,1024]{2,1,0:T(4,128)}, s32[8,4,1024]{2,1,0:T(4,128)S(1)}, u32[]{:S(2)}, u32[]{:S(2)}) collective-permute-start(s32[8,4,1024]{2,1,0:T(4,128)} %get-tuple-element.49), channel_id=1, source_target_pairs={{0,1},{1,2},{2,3},{3,4},{4,5},{5,6},{6,7},{8,9},{9,10},{10,11},{11... | collective-permute-start | bytes 393224 | tf_op jit(solution)/shard_map/ppermute | solution.py:636
  28.9 40.3 %collective-permute-start.4 = (s32[64,1024]{1,0:T(8,128)}, s32[64,1024]{1,0:T(8,128)S(1)}, u32[]{:S(2)}, u32[]{:S(2)}) collective-permute-start(s32[64,1024]{1,0:T(8,128)} %get-tuple-element.55), channel_id=1, source_target_pairs={{8,0},{16,8},{24,16},{32,24},{40,32},{48,40},{56,48},{64,56},{72,6... | collective-permute-start | bytes 786440 | tf_op jit(solution)/shard_map/ppermute | solution.py:636
  58.9 14.0 %collective-permute-start.2 = (f32[768,128]{1,0:T(8,128)S(1)}, f32[768,128]{1,0:T(8,128)S(1)}, u32[]{:S(2)}, u32[]{:S(2)}) collective-permute-start(f32[768,128]{1,0:T(8,128)S(1)} %get-tuple-element.51), channel_id=1, source_target_pairs={{1,0},{2,1},{3,2},{4,3},{5,4},{6,5},{7,6},{9,8},{10,9},{11,10},{12... | collective-permute-start | bytes 1179656 | tf_op jit(solution)/shard_map/ppermute | solution.py:636
  62.4 10.5 %collective-permute-start.3 = (f32[768,128]{1,0:T(8,128)S(1)}, f32[768,128]{1,0:T(8,128)S(1)}, u32[]{:S(2)}, u32[]{:S(2)}) collective-permute-start(f32[768,128]{1,0:T(8,128)S(1)} %get-tuple-element.52), channel_id=1, source_target_pairs={{0,1},{1,2},{2,3},{3,4},{4,5},{5,6},{6,7},{8,9},{9,10},{10,11},{11... | collective-permute-start | bytes 1179656 | tf_op jit(solution)/shard_map/ppermute | solution.py:636
  64.5 4.7 %collective-permute-start.5 = (s32[8,1024]{1,0:T(8,128)S(1)}, s32[8,1024]{1,0:T(8,128)S(1)}, u32[]{:S(2)}, u32[]{:S(2)}) collective-permute-start(s32[8,1024]{1,0:T(8,128)S(1)} %fusion.1), channel_id=1, source_target_pairs={{8,0},{16,8},{24,16},{32,24},{40,32},{48,40},{56,48},{64,56},{72,6... | collective-permute-start | bytes 98312 | tf_op jit(solution)/shard_map/ppermute | solution.py:636
  73.9 6.8 %collective-permute-start.6 = (f32[72,1024]{1,0:T(8,128)S(1)}, f32[72,1024]{1,0:T(8,128)S(1)}, u32[]{:S(2)}, u32[]{:S(2)}) collective-permute-start(f32[72,1024]{1,0:T(8,128)S(1)} %get-tuple-element.63), channel_id=1, source_target_pairs={{0,8},{8,16},{16,24},{24,32},{32,40},{40,48},{48,56},{56,64},{64,7... | collective-permute-start | bytes 884744 | tf_op jit(solution)/shard_map/ppermute | solution.py:636
  75.6 9.0 %collective-permute-start.7 = (f32[72,1024]{1,0:T(8,128)S(1)}, f32[72,1024]{1,0:T(8,128)S(1)}, u32[]{:S(2)}, u32[]{:S(2)}) collective-permute-start(f32[72,1024]{1,0:T(8,128)S(1)} %get-tuple-element.64), channel_id=1, source_target_pairs={{8,0},{16,8},{24,16},{32,24},{40,32},{48,40},{56,48},{64,56},{72,6... | collective-permute-start | bytes 884744 | tf_op jit(solution)/shard_map/ppermute | solution.py:636
  85.3 10.9 %collective-permute-start.8 = (f32[72,1024]{1,0:T(8,128)S(1)}, f32[72,1024]{1,0:T(8,128)S(1)}, u32[]{:S(2)}, u32[]{:S(2)}) collective-permute-start(f32[72,1024]{1,0:T(8,128)S(1)} %get-tuple-element.70), channel_id=1, source_target_pairs={{0,8},{8,16},{16,24},{24,32},{32,40},{40,48},{48,56},{56,64},{64,7... | collective-permute-start | bytes 884744 | tf_op jit(solution)/shard_map/ppermute | solution.py:636
  91.1 8.9 %collective-permute-start.9 = (f32[72,1024]{1,0:T(8,128)S(1)}, f32[72,1024]{1,0:T(8,128)S(1)}, u32[]{:S(2)}, u32[]{:S(2)}) collective-permute-start(f32[72,1024]{1,0:T(8,128)S(1)} %get-tuple-element.71), channel_id=1, source_target_pairs={{8,0},{16,8},{24,16},{32,24},{40,32},{48,40},{56,48},{64,56},{72,6... | collective-permute-start | bytes 884744 | tf_op jit(solution)/shard_map/ppermute | solution.py:636
  100.9 11.7 %collective-permute-start.10 = (f32[72,1024]{1,0:T(8,128)S(1)}, f32[72,1024]{1,0:T(8,128)S(1)}, u32[]{:S(2)}, u32[]{:S(2)}) collective-permute-start(f32[72,1024]{1,0:T(8,128)S(1)} %get-tuple-element.77), channel_id=1, source_target_pairs={{0,8},{8,16},{16,24},{24,32},{32,40},{40,48},{48,56},{56,64},{64,7... | collective-permute-start | bytes 884744 | tf_op jit(solution)/shard_map/ppermute | solution.py:636
  104.9 7.9 %collective-permute-start.11 = (f32[72,1024]{1,0:T(8,128)S(1)}, f32[72,1024]{1,0:T(8,128)S(1)}, u32[]{:S(2)}, u32[]{:S(2)}) collective-permute-start(f32[72,1024]{1,0:T(8,128)S(1)} %get-tuple-element.78), channel_id=1, source_target_pairs={{8,0},{16,8},{24,16},{32,24},{40,32},{48,40},{56,48},{64,56},{72,6... | collective-permute-start | bytes 884744 | tf_op jit(solution)/shard_map/ppermute | solution.py:636
  116.5 40.7 %copy-start.1 = (f32[512,3,128]{2,0,1:T(8,128)S(1)}, f32[512,3,128]{2,0,1:T(8,128)}, u32[]{:S(2)}) copy-start(f32[512,3,128]{2,0,1:T(8,128)} %param.6) | copy-start | bytes 2359300
  116.5 40.6 %copy-start.2 = (s32[512,128]{1,0:T(8,128)S(1)}, s32[512,128]{1,0:T(8,128)}, u32[]{:S(2)}) copy-start(s32[512,128]{1,0:T(8,128)} %offset.1) | copy-start | bytes 786436
  116.5 40.6 %copy-start.3 = (s32[512]{0:T(512)S(1)}, s32[512]{0:T(512)}, u32[]{:S(2)}) copy-start(s32[512]{0:T(512)} %get-tuple-element.88.place) | copy-start | bytes 6148
